TPU v7x, 128 devices: a whole 4x4x4 slice. The times are simulated.
128 devices in a mesh: lat: 16 (over y, z), ch: 8 (over x, core).
Axes of the slice: x: 4, y: 4, z: 4, core: 2. Of those that a mesh axis runs over, the one named last changes fastest.
Arguments:
- field_in: bfloat16 [768, 384, 768], P('ch', 'lat'), may hold values from -80 to 80
- ln_gain: float32 [2, 768], P(None, 'ch'), may hold values from 0.5 to 1.5
- ln_shift: float32 [2, 768], P(None, 'ch'), may hold values from -1.5 to 1.5
- mix_first: bfloat16 [2, 2, 8, 96, 96], P(None, None, 'ch'), may hold values from -0.4375 to 0.4375
- mix_bias: bfloat16 [2, 2, 8, 96], P(None, None, 'ch'), may hold values from -3 to 3
- mix_second: bfloat16 [2, 2, 8, 96, 96], P(None, None, 'ch'), may hold values from -0.4375 to 0.4375
Outputs:
- field_out: bfloat16 [768, 384, 768], P('ch', 'lat')
All inputs are finite; a program needn't handle non-finite values.
Results may differ from a plain program's by a relative error of at most 0.014.
Values may be sent and summed in bfloat16 or wider, within the bound.
No kernel may reach another device: no remote copies, remote signals or barrier semaphores. Data moves between devices by JAX's collectives and lax.ppermute only.
A program may use at most 128 MiB of HBM per device.

v0:
```python
import functools
import math

import jax
import jax.numpy as jnp
from jax import lax
from jax.sharding import Mesh
from jax.sharding import PartitionSpec as P

CH = ("ch_0", "ch_1")
LAT = ("lat_0", "lat_1")
LAT_CH = ("lat_0", "lat_1", "ch_0", "ch_1")


norm_eps = 1e-05
shrink_level = 0.01


def copy_for_each(x, axis):
    copies = jnp.broadcast_to(x, (lax.axis_size(axis), *x.shape))
    return lax.all_to_all(copies, axis, split_axis=0, concat_axis=0, tiled=True)


def taken_together(x, axis):
    everything = copy_for_each(x, axis)
    return jnp.sum(everything.astype(jnp.float32), axis=0)


def by_axis(x, axes):
    return functools.reduce(lax.psum, axes, x)


def soft_shrink(values):
    return jnp.sign(values) * jnp.maximum(jnp.abs(values) - shrink_level, 0.0)


def trig_angles(length, freq_ids):
    positions = jnp.arange(length, dtype=jnp.int32)
    phase_ids = positions[:, None] * freq_ids[None, :] % length
    angles = phase_ids.astype(jnp.float32) * (2.0 * math.pi / length)
    norm_scale = 1.0 / math.sqrt(length)
    return (jnp.cos(angles) * norm_scale, jnp.sin(angles) * norm_scale)


def lon_tables(lon_cells, pieces):
    mode_count = lon_cells // 2
    per_piece = mode_count // pieces
    column = jnp.arange(2 * mode_count, dtype=jnp.int32)
    is_imag = column // per_piece % 2
    freq_ids = column // (2 * per_piece) * per_piece + column % per_piece
    cos_part, sin_part = trig_angles(lon_cells, freq_ids)
    forward = jnp.where(is_imag[None, :] == 0, cos_part, -sin_part).astype(jnp.bfloat16)
    weight_k = jnp.where(freq_ids == 0, 1.0, 2.0).astype(jnp.float32)
    inverse = (forward.astype(jnp.float32).T * weight_k[:, None]).astype(jnp.bfloat16)
    return (forward, inverse)


def normalize(source, gain, shift):
    ch_all = source.shape[0] * lax.axis_size(CH)
    total_sum, squares = (
        taken_together(jnp.sum(source, axis=0).astype(jnp.bfloat16), CH).astype(jnp.float32),
        taken_together(jnp.sum(source * source, axis=0).astype(jnp.bfloat16), CH).astype(
            jnp.float32
        ),
    )
    mean_val = total_sum / ch_all
    spread = squares / ch_all - mean_val * mean_val
    inv_std = lax.rsqrt(spread + norm_eps)
    gain_col = gain[:, None, None]
    shift_col = shift[:, None, None]
    return ((source - mean_val) * inv_std * gain_col + shift_col).astype(jnp.bfloat16)


def lat_transform(mode_data, cos_lat, sin_lat, backward):
    chans, lat_rows, width_q = mode_data.shape
    part_cos = jnp.einsum("hj,chq->cjq", cos_lat, mode_data, preferred_element_type=jnp.float32)
    part_sin = jnp.einsum("hj,chq->cjq", sin_lat, mode_data, preferred_element_type=jnp.float32)
    part_cos = part_cos.reshape(chans, lat_rows, 2, width_q // 2)
    part_sin = part_sin.reshape(chans, lat_rows, 2, width_q // 2)
    if backward:
        real_part = part_cos[:, :, 0] - part_sin[:, :, 1]
        imag_part = part_cos[:, :, 1] + part_sin[:, :, 0]
    else:
        real_part = part_cos[:, :, 0] + part_sin[:, :, 1]
        imag_part = part_cos[:, :, 1] - part_sin[:, :, 0]
    return jnp.stack([real_part, imag_part], axis=2).astype(jnp.bfloat16)


def contract(operand, weight):
    return jnp.einsum("bcjm,bcd->bdjm", operand, weight, preferred_element_type=jnp.float32)


def block_mix(lat_spec, first_w, first_b, second_w, block_width):
    chans, lat_rows, two_parts, per_piece = lat_spec.shape
    block_count = chans // block_width
    grouped = lat_spec.reshape(block_count, block_width, lat_rows, two_parts, per_piece)
    spec_re = grouped[:, :, :, 0]
    spec_im = grouped[:, :, :, 1]
    bias_f = first_b.astype(jnp.float32)
    hid_re = jax.nn.relu(
        contract(spec_re, first_w[0]) - contract(spec_im, first_w[1]) + bias_f[0][:, :, None, None]
    ).astype(jnp.bfloat16)
    hid_im = jax.nn.relu(
        contract(spec_im, first_w[0]) + contract(spec_re, first_w[1]) + bias_f[1][:, :, None, None]
    ).astype(jnp.bfloat16)
    mix_re = soft_shrink(contract(hid_re, second_w[0]) - contract(hid_im, second_w[1])).astype(
        jnp.bfloat16
    )
    mix_im = soft_shrink(contract(hid_im, second_w[0]) + contract(hid_re, second_w[1])).astype(
        jnp.bfloat16
    )
    return jnp.stack([mix_re, mix_im], axis=3).reshape(chans, lat_rows, two_parts * per_piece)


def per_device(field_in, ln_gain, ln_shift, mix_first, mix_bias, mix_second):
    lat_parts = lax.axis_size(LAT)
    ch_dev, band_rows, lon_cells = field_in.shape
    lat_rows = band_rows * lat_parts
    block_width = mix_first.shape[-1]
    first_all, bias_all, second_all = (mix_first, mix_bias, mix_second)
    per_piece = lon_cells // 2 // lat_parts
    forward, inverse = lon_tables(lon_cells, lat_parts)
    cos_f, sin_f = trig_angles(lat_rows, jnp.arange(lat_rows, dtype=jnp.int32))
    cos_lat = cos_f.astype(jnp.bfloat16)
    sin_lat = sin_f.astype(jnp.bfloat16)
    row_pos = (lax.axis_index(LAT) * band_rows + jnp.arange(band_rows, dtype=jnp.int32)).astype(
        jnp.float32
    )
    area_weights = jnp.cos((row_pos + 0.5) * (math.pi / lat_rows) - 0.5 * math.pi)[None, :, None]
    source = field_in.astype(jnp.float32)
    target = by_axis(jnp.sum(area_weights * source * source), LAT_CH)
    current = field_in
    for layer_idx in range(mix_first.shape[0]):
        normed = normalize(source, ln_gain[layer_idx], ln_shift[layer_idx])
        lon_spec = jnp.dot(
            normed.reshape(ch_dev * band_rows, lon_cells),
            forward,
            preferred_element_type=jnp.float32,
        ).astype(jnp.bfloat16)
        mode_data = lax.all_to_all(
            lon_spec.reshape(ch_dev, band_rows, lon_cells),
            LAT,
            split_axis=2,
            concat_axis=1,
            tiled=True,
        )
        lat_spec = lat_transform(mode_data, cos_lat, sin_lat, False)
        mixed_spec = block_mix(
            lat_spec, first_all[layer_idx], bias_all[layer_idx], second_all[layer_idx], block_width
        )
        back_spec = lat_transform(mixed_spec, cos_lat, sin_lat, True).reshape(
            ch_dev, lat_rows, 2 * per_piece
        )
        band_spec = lax.all_to_all(back_spec, LAT, split_axis=1, concat_axis=2, tiled=True)
        spatial = jnp.dot(
            band_spec.reshape(ch_dev * band_rows, lon_cells),
            inverse,
            preferred_element_type=jnp.float32,
        )
        spatial = spatial.reshape(ch_dev, band_rows, lon_cells)
        summed = spatial + normed.astype(jnp.float32) + current.astype(jnp.float32)
        energy = by_axis(jnp.sum(area_weights * summed * summed), LAT_CH)
        current = (summed * jnp.sqrt(target / energy)).astype(jnp.bfloat16)
        source = current.astype(jnp.float32)
    return current


def solution(mesh):
    finer = Mesh(mesh.devices.reshape(4, 4, 4, 2), ("lat_0", "lat_1", "ch_0", "ch_1"))
    in_specs = (
        P(CH, LAT, None),
        P(None, CH),
        P(None, CH),
        P(None, None, CH, None, None),
        P(None, None, CH, None),
        P(None, None, CH, None, None),
    )
    out_specs = P(CH, LAT, None)
    return jax.shard_map(
        per_device, mesh=finer, in_specs=in_specs, out_specs=out_specs, check_vma=False
    )
```

profile of v0, /device:TPU:1, one launch (start us, length us, event | category | flops | bytes accessed | tf_op | source)
XLA Modules:
  0.0 625.2 jit_solution(16360192033380045489)
XLA Ops:
  4.8 5.8 all-to-all-start
  11.9 5.5 all-to-all-done
  19.0 5.0 all-to-all-start.1
  26.8 4.1 all-to-all-done.1
  34.2 15.9 %convolution_convert_fusion.1 = bf16[2304,768]{1,0:T(8,128)(2,1)} fusion(bf16[2304,768]{1,0:T(8,128)(2,1)S(1)} %bitcast.246, s32[768]{0:T(1024)S(1)} %copy-done.12, pred[768]{0:T(1024)(128)(4,1)S(1)} %copy-done.21), kind=kOutput, calls=%fused_computation.26 | convolution fusion | flops 2727936000 | bytes 7081728 | tf_op jit(solution)/shard_map/dot_general | solution.py:135
  50.2 7.1 %copy.99 = bf16[96,24,768]{0,1,2:T(8,128)(2,1)} copy(bf16[96,24,768]{2,1,0:T(8,128)(2,1)} %bitcast.244) | data formatting | bytes 7077888 | tf_op jit(solution)/shard_map/reshape | solution.py:141
  57.3 7.8 %all-to-all-start.2 = ((bf16[96,24,768]{0,1,2:T(8,128)(2,1)}), bf16[96,24,768]{0,1,2:T(8,128)(2,1)}, u32[]{:S(2)}, u32[]{:S(2)}) async-start(bf16[96,24,768]{0,1,2:T(8,128)(2,1)} %copy.99), calls=%async_computation.2 | async-start | bytes 9437184 | tf_op jit(solution)/shard_map/all_to_all | solution.py:140
  66.3 68.7 %all-to-all-done.2 = bf16[96,24,768]{0,1,2:T(8,128)(2,1)} async-done(((bf16[96,24,768]{0,1,2:T(8,128)(2,1)}), bf16[96,24,768]{0,1,2:T(8,128)(2,1)}, u32[]{:S(2)}, u32[]{:S(2)}) %all-to-all-start.2) | async-done | bytes 3538976 | tf_op jit(solution)/shard_map/all_to_all | solution.py:140
  135.0 5.6 copy.101
  140.6 7.4 %copy.102 = bf16[96,384,48]{1,2,0:T(8,128)(2,1)} copy(bf16[96,384,48]{0,2,1:T(8,128)(2,1)} %bitcast.239) | data formatting | bytes 7077888 | tf_op jit(solution)/shard_map/all_to_all | solution.py:140
  148.0 6.2 fusion.85
  154.3 4.1 fusion.91
  170.3 4.5 fusion.25
  174.8 4.9 fusion.27
  182.3 4.2 pad_maximum_fusion.1
  186.5 7.1 %copy.114 = bf16[96,384,2,24]{0,3,2,1:T(8,128)(2,1)} copy(bf16[96,384,2,24]{1,3,2,0:T(8,128)(2,1)} %pad_maximum_fusion.1) | data formatting | bytes 7077888 | tf_op jit(solution)/shard_map/stack | solution.py:86
  193.7 8.6 %all-to-all-start.3 = ((bf16[96,384,48]{0,2,1:T(8,128)(2,1)}), bf16[96,384,48]{0,2,1:T(8,128)(2,1)}, u32[]{:S(2)}, u32[]{:S(2)}) async-start(bf16[96,384,48]{0,2,1:T(8,128)(2,1)} %bitcast.238), calls=%async_computation.3 | async-start | bytes 9437184 | tf_op jit(solution)/shard_map/all_to_all | solution.py:154
  203.5 55.3 %all-to-all-done.3 = bf16[96,384,48]{0,2,1:T(8,128)(2,1)} async-done(((bf16[96,384,48]{0,2,1:T(8,128)(2,1)}), bf16[96,384,48]{0,2,1:T(8,128)(2,1)}, u32[]{:S(2)}, u32[]{:S(2)}) %all-to-all-start.3) | async-done | bytes 3538976 | tf_op jit(solution)/shard_map/all_to_all | solution.py:154
  258.8 5.8 copy.115
  264.6 6.7 %copy.116 = bf16[96,24,768]{2,1,0:T(8,128)(2,1)} copy(bf16[96,24,768]{0,2,1:T(8,128)(2,1)} %bitcast.240) | data formatting | bytes 7077888 | tf_op jit(solution)/shard_map/dot_general | solution.py:155
  271.3 20.3 %fusion = (f32[]{:T(128)}, f32[]{:T(128)}, f32[96,24,768]{2,1,0:T(8,128)}) fusion(f32[24]{0:T(128)} %add_cosine_fusion, bf16[96,24,768]{2,1,0:T(8,128)(2,1)S(1)} %copy-done, f32[96]{0:T(128)S(1)} %get-tuple-element.40, f32[96]{0:T(128)S(1)} %get-tuple-element.46, f32[24,768]{1,0:T(8,128)} %copy-done.5, f32[24,768]{1,0:T(8,128)} %copy-done.4, ...), kind=kOutput, calls=%fused_computation.10 | convolution fusion | flops 2754478080 | bytes 14311016 | tf_op jit(solution)/shard_map/dot_general | solution.py:155
  291.6 6.6 %all-reduce.2 = (f32[]{:T(128)}, f32[]{:T(128)}) all-reduce(f32[]{:T(128)} %get-tuple-element.6, f32[]{:T(128)} %get-tuple-element.5), channel_id=1, replica_groups=mesh['lat_0'=4,'lat_1'=4,'ch_0'=4,'ch_1'=2] {'lat_0'}, use_global_device_ids=true, to_apply=%region_5.6 | all-reduce | flops 2 | bytes 16 | tf_op jit(solution)/shard_map/psum | solution.py:30
  298.3 11.6 %all-reduce.1 = (f32[]{:T(128)}, f32[]{:T(128)}) all-reduce(f32[]{:T(128)} %get-tuple-element.11, f32[]{:T(128)} %get-tuple-element.12), channel_id=1, replica_groups=mesh['lat_0'=4,'lat_1'=4,'ch_0'=4,'ch_1'=2] {'lat_1'}, use_global_device_ids=true, to_apply=%region_6.7 | all-reduce | flops 2 | bytes 16 | tf_op jit(solution)/shard_map/psum | solution.py:30
  309.9 11.0 %all-reduce = (f32[]{:T(128)}, f32[]{:T(128)}) all-reduce(f32[]{:T(128)} %get-tuple-element.9, f32[]{:T(128)} %get-tuple-element.10), channel_id=1, replica_groups=mesh['lat_0'=4,'lat_1'=4,'ch_0'=4,'ch_1'=2] {'ch_0'}, use_global_device_ids=true, to_apply=%region_7.8 | all-reduce | flops 2 | bytes 16 | tf_op jit(solution)/shard_map/psum | solution.py:30
  320.9 11.2 %all-reduce.3 = (f32[]{:T(128)}, f32[]{:T(128)}) all-reduce(f32[]{:T(128)} %get-tuple-element.7, f32[]{:T(128)} %get-tuple-element.8), channel_id=1, replica_groups=mesh['lat_0'=4,'lat_1'=4,'ch_0'=4,'ch_1'=2] {'ch_1'}, use_global_device_ids=true, to_apply=%region_8.9 | all-reduce | flops 2 | bytes 16 | tf_op jit(solution)/shard_map/psum | solution.py:30
  333.5 4.9 fusion.190
  340.9 10.7 %all_to_all.86 = bf16[8,24,768]{2,1,0:T(8,128)(2,1)S(1)} all-to-all(bf16[8,24,768]{2,1,0:T(8,128)(2,1)S(1)} %broadcast_in_dim.52), channel_id=1, replica_groups=mesh['lat_0'=4,'lat_1'=4,'ch_0'=4,'ch_1'=2] {'ch_0','ch_1'}, dimensions={0} | all-to-all | bytes 589824 | tf_op jit(solution)/shard_map/all_to_all | solution.py:21
  352.3 3.9 all-to-all-start.4
  356.2 6.8 %all-to-all-done.4 = bf16[8,24,768]{2,1,0:T(8,128)(2,1)S(1)} async-done(((bf16[8,24,768]{2,1,0:T(8,128)(2,1)}), bf16[8,24,768]{2,1,0:T(8,128)(2,1)S(1)}, u32[]{:S(2)}, u32[]{:S(2)}) %all-to-all-start.4) | async-done | bytes 294944 | tf_op jit(solution)/shard_map/all_to_all | solution.py:21
  363.1 3.4 fusion.4
  366.5 15.1 %convolution_convert_fusion = bf16[2304,768]{1,0:T(8,128)(2,1)S(1)} fusion(bf16[2304,768]{1,0:T(8,128)(2,1)S(1)} %bitcast.247, s32[768]{0:T(1024)S(1)} %copy-done.13, pred[768]{0:T(1024)(128)(4,1)S(1)} %copy-done.22), kind=kOutput, calls=%fused_computation.25 | convolution fusion | flops 2727936000 | bytes 7081728 | tf_op jit(solution)/shard_map/dot_general | solution.py:135
  381.6 5.1 copy.117
  386.7 58.5 %all_to_all.87 = bf16[96,24,768]{0,1,2:T(8,128)(2,1)S(1)} all-to-all(bf16[96,24,768]{0,1,2:T(8,128)(2,1)} %copy.117), channel_id=1, replica_groups=mesh['lat_0'=4,'lat_1'=4,'ch_0'=4,'ch_1'=2] {'lat_0','lat_1'}, dimensions={2} | all-to-all | bytes 7077888 | tf_op jit(solution)/shard_map/all_to_all | solution.py:140
  448.3 6.4 %copy.120 = bf16[96,384,48]{1,2,0:T(8,128)(2,1)S(1)} copy(bf16[96,384,48]{0,2,1:T(8,128)(2,1)} %bitcast.241) | data formatting | bytes 7077888 | tf_op jit(solution)/shard_map/all_to_all | solution.py:140
  454.7 4.1 fusion.82
  458.8 4.1 fusion.88
  474.8 4.4 fusion.21
  479.3 4.8 fusion.23
  489.2 5.3 copy.132
  494.5 58.4 %all_to_all.88 = bf16[96,384,48]{0,2,1:T(8,128)(2,1)S(1)} all-to-all(bf16[96,384,48]{0,2,1:T(8,128)(2,1)} %bitcast.242), channel_id=1, replica_groups=mesh['lat_0'=4,'lat_1'=4,'ch_0'=4,'ch_1'=2] {'lat_0','lat_1'}, dimensions={1} | all-to-all | bytes 7077888 | tf_op jit(solution)/shard_map/all_to_all | solution.py:154
  552.8 3.4 copy.133
  556.2 7.0 %copy.134 = bf16[96,24,768]{2,1,0:T(8,128)(2,1)} copy(bf16[96,24,768]{0,2,1:T(8,128)(2,1)} %bitcast.243) | data formatting | bytes 7077888 | tf_op jit(solution)/shard_map/dot_general | solution.py:155
  563.3 19.7 %fusion.6 = (f32[]{:T(128)}, f32[96,24,768]{2,1,0:T(8,128)}) fusion(f32[24]{0:T(128)} %add_cosine_fusion, bf16[96,24,768]{2,1,0:T(8,128)(2,1)S(1)} %copy-done.2, f32[96]{0:T(128)S(1)} %get-tuple-element.39, f32[96]{0:T(128)S(1)} %get-tuple-element.47, f32[24,768]{1,0:T(8,128)} %copy-done.7, f32[24,768]{1,0:T(8,128)} %copy-done.6, ...), kind=kOutput, calls=%fused_computation.16 | convolution fusion | flops 2749169664 | bytes 14311012 | tf_op jit(solution)/shard_map/dot_general | solution.py:155
  582.9 8.4 %psum.92 = f32[]{:T(128)} all-reduce(f32[]{:T(128)} %get-tuple-element.44), channel_id=1, replica_groups=mesh['lat_0'=4,'lat_1'=4,'ch_0'=4,'ch_1'=2] {'lat_0'}, use_global_device_ids=true, to_apply=%region_19.20 | all-reduce | flops 1 | bytes 8 | tf_op jit(solution)/shard_map/psum | solution.py:30
  591.4 6.9 %psum.93 = f32[]{:T(128)} all-reduce(f32[]{:T(128)} %psum.92), channel_id=1, replica_groups=mesh['lat_0'=4,'lat_1'=4,'ch_0'=4,'ch_1'=2] {'lat_1'}, use_global_device_ids=true, to_apply=%region_20.21 | all-reduce | flops 1 | bytes 8 | tf_op jit(solution)/shard_map/psum | solution.py:30
  598.2 7.5 %psum.94 = f32[]{:T(128)} all-reduce(f32[]{:T(128)} %psum.93), channel_id=1, replica_groups=mesh['lat_0'=4,'lat_1'=4,'ch_0'=4,'ch_1'=2] {'ch_0'}, use_global_device_ids=true, to_apply=%region_21.22 | all-reduce | flops 1 | bytes 8 | tf_op jit(solution)/shard_map/psum | solution.py:30
  605.7 12.1 %psum.95 = f32[]{:T(128)} all-reduce(f32[]{:T(128)} %psum.94), channel_id=1, replica_groups=mesh['lat_0'=4,'lat_1'=4,'ch_0'=4,'ch_1'=2] {'ch_1'}, use_global_device_ids=true, to_apply=%region_22.23 | all-reduce | flops 1 | bytes 8 | tf_op jit(solution)/shard_map/psum | solution.py:30
  619.2 5.7 multiply_convert_fusion
  (97 shorter events, 54.0 us)
Async XLA Ops:
  0.0 10.6 %copy-start = (bf16[96,24,768]{2,1,0:T(8,128)(2,1)S(1)}, bf16[96,24,768]{2,1,0:T(8,128)(2,1)}, u32[]{:S(2)}) copy-start(bf16[96,24,768]{2,1,0:T(8,128)(2,1)} %param.6) | copy-start | bytes 10616836
  4.8 12.7 %all-to-all-start = ((bf16[8,24,768]{2,1,0:T(8,128)(2,1)}), bf16[8,24,768]{2,1,0:T(8,128)(2,1)}, u32[]{:S(2)}, u32[]{:S(2)}) async-start(bf16[8,24,768]{2,1,0:T(8,128)(2,1)} %broadcast_in_dim.45), calls=%async_computation | async-start | bytes 589824 | tf_op jit(solution)/shard_map/all_to_all | solution.py:21
  10.6 1.4 copy-start.19
  10.6 1.4 copy-start.20
  19.0 11.9 %all-to-all-start.1 = ((bf16[8,24,768]{2,1,0:T(8,128)(2,1)}), bf16[8,24,768]{2,1,0:T(8,128)(2,1)}, u32[]{:S(2)}, u32[]{:S(2)}) async-start(bf16[8,24,768]{2,1,0:T(8,128)(2,1)} %broadcast_in_dim.46), calls=%async_computation.1 | async-start | bytes 589824 | tf_op jit(solution)/shard_map/all_to_all | solution.py:21
  32.8 1.4 copy-start.4
  32.8 1.4 copy-start.5
  32.8 1.4 copy-start.12
  32.9 1.4 copy-start.21
  57.3 77.8 %all-to-all-start.2 = ((bf16[96,24,768]{0,1,2:T(8,128)(2,1)}), bf16[96,24,768]{0,1,2:T(8,128)(2,1)}, u32[]{:S(2)}, u32[]{:S(2)}) async-start(bf16[96,24,768]{0,1,2:T(8,128)(2,1)} %copy.99), calls=%async_computation.2 | async-start | bytes 9437184 | tf_op jit(solution)/shard_map/all_to_all | solution.py:140
  148.0 6.3 %copy-start.3 = (bf16[96,384,48]{1,2,0:T(8,128)(2,1)S(1)}, bf16[96,384,48]{1,2,0:T(8,128)(2,1)}, u32[]{:S(2)}) copy-start(bf16[96,384,48]{1,2,0:T(8,128)(2,1)} %copy.102) | copy-start | bytes 10616836
  160.6 1.2 copy-start.8
  162.7 0.7 copy-start.18
  163.4 0.7 copy-start.17
  164.0 0.9 copy-start.10
  193.7 65.1 %all-to-all-start.3 = ((bf16[96,384,48]{0,2,1:T(8,128)(2,1)}), bf16[96,384,48]{0,2,1:T(8,128)(2,1)}, u32[]{:S(2)}, u32[]{:S(2)}) async-start(bf16[96,384,48]{0,2,1:T(8,128)(2,1)} %bitcast.238), calls=%async_computation.3 | async-start | bytes 9437184 | tf_op jit(solution)/shard_map/all_to_all | solution.py:154
  338.3 1.8 copy-start.1
  352.3 10.7 %all-to-all-start.4 = ((bf16[8,24,768]{2,1,0:T(8,128)(2,1)}), bf16[8,24,768]{2,1,0:T(8,128)(2,1)S(1)}, u32[]{:S(2)}, u32[]{:S(2)}) async-start(bf16[8,24,768]{2,1,0:T(8,128)(2,1)} %broadcast_in_dim.51), calls=%async_computation.4 | async-start | bytes 589824 | tf_op jit(solution)/shard_map/all_to_all | solution.py:21
  363.1 3.4 copy-start.6
  363.1 3.4 copy-start.7
  363.1 3.4 copy-start.13
  363.1 3.4 copy-start.22
  463.9 1.2 copy-start.9
  467.2 0.7 copy-start.16
  467.8 0.9 copy-start.11
  468.7 0.7 copy-start.15
  556.2 7.0 %copy-start.2 = (bf16[96,24,768]{2,1,0:T(8,128)(2,1)S(1)}, bf16[96,24,768]{2,1,0:T(8,128)(2,1)}, u32[]{:S(2)}) copy-start(bf16[96,24,768]{2,1,0:T(8,128)(2,1)} %copy-done.1) | copy-start | bytes 10616836
  556.2 7.0 %copy-start.14 = (f32[768]{0:T(1024)S(1)}, f32[768]{0:T(1024)}, u32[]{:S(2)}) copy-start(f32[768]{0:T(1024)} %compare_select_fusion) | copy-start | bytes 9220
where the time goes:
time: 633 us; the launch traced here: 625 us
  blocking collectives  203 us (32%)
  waiting for transfers between devices  140 us (22%)
  matrix products  124 us (20%)
  local copies, waits for them, and re-layouts  78.5 us (12%)
  other arithmetic  45.1 us (7%)
  starting transfers between devices  31.1 us (5%)
    psum x8, blocking collectives, by_axis(): return functools.reduce(lax.psum, axes, x)  75.4 us
    all_to_all x1, waiting for transfers between devices, per_device(): lax.all_to_all(lon_spec.reshape(ch_dev, band_rows, lon_cells), LAT, split...  68.7 us
    all_to_all x1, blocking collectives, per_device(): lax.all_to_all(lon_spec.reshape(ch_dev, band_rows, lon_cells), LAT, split...  58.5 us
    all_to_all x1, blocking collectives, per_device(): lax.all_to_all(back_spec, LAT, split_axis=1, concat_axis=2, tiled=True)  58.4 us
    all_to_all x1, waiting for transfers between devices, per_device(): lax.all_to_all(back_spec, LAT, split_axis=1, concat_axis=2, tiled=True)  55.3 us
    dot_general x2, matrix products, per_device(): jnp.dot(band_spec.reshape(ch_dev * band_rows, lon_cells), inverse, prefer...  40 us
    dot_general x2, matrix products, per_device(): jnp.dot(normed.reshape(ch_dev * band_rows, lon_cells), forward, preferred...  31 us
    all_to_all x4, local copies, waits for them, and re-layouts, per_device(): lax.all_to_all(lon_spec.reshape(ch_dev, band_rows, lon_cells), LAT, split...  22.5 us
  transfers between devices with their start and end apart: 5, of which 5 were waited for; matrix products, arithmetic and copies ran while one was open for 1% of the time, Pallas kernels for 0%

commit v1 on v0

v1 whole, which is shorter than its diff:
```python
import functools
import math

import jax
import jax.numpy as jnp
import numpy as np
from jax import lax
from jax.experimental import pallas as pl
from jax.experimental.pallas import tpu as pltpu
from jax.sharding import Mesh
from jax.sharding import PartitionSpec as P

CH = ("ch_0", "ch_1")
LAT = ("lat_0", "lat_1")
LAT_CH = LAT + CH
NORM_EPS = 1e-05


def host_tables():
    def trig(length, freqs):
        n = np.arange(length)
        a = (n[:, None] * freqs[None, :] % length) * (2.0*math.pi/length)
        s = 1.0/math.sqrt(length)
        bf = jnp.bfloat16
        return (np.cos(a)*s).astype(bf), (np.sin(a)*s).astype(bf)
    c, s = trig(384, np.arange(384))
    tf = np.concatenate([c, s], 1)
    re = np.concatenate([c.T, -s.T], 1).reshape(16, 24, 768)
    im = np.concatenate([s.T, c.T], 1).reshape(16, 24, 768)
    ti = np.stack([re, im], 1).reshape(768, 768)
    lc, ls = trig(768, np.arange(384))
    t = np.concatenate([lc.T, -ls.T], 0)
    return tf, ti, t


def exchange_into(xs, unit, put):
    for c in range(len(xs)):
        put(c, jnp.concatenate([x[:, unit*c:unit*(c+1)] for x in xs], axis=1))

def dot(a, b, dims=((1,),(0,))):
    return lax.dot_general(a, b, (dims, ((),())), preferred_element_type=jnp.float32)

def spectral_kernel(r_ref, w1_ref, b1_ref, w2_ref, tf_ref, ti_ref, o_ref, g_ref, f_ref, h_ref):
    n_band, rows, lanes = r_ref.shape
    groups = lanes // 384
    def forward(g, _):
        l = pl.ds(pl.multiple_of(g*384, 384), 384)
        for t in range(rows//16):
            xs = [r_ref[p, 16*t:16*t+16, l] for p in range(16)]
            def put(c, v, t=t):
                g_ref[48*c+16*t:48*c+16*t+16, :] = v
            exchange_into(xs, 24, put)
        prod = dot(g_ref[...], tf_ref[...]).reshape(16, 48, 768)
        re, im = prod[:, :24], prod[:, 24:]
        row = pl.ds(pl.multiple_of(g*384, 384), 384)
        for k in range(3):
            a, b = slice(128*k, 128*k+128), slice(384+128*k, 512+128*k)
            f_ref[k, row, :] = (re[:, :, a] + im[:, :, b]).reshape(384, 128)
            f_ref[3+k, row, :] = (im[:, :, a] - re[:, :, b]).reshape(384, 128)
        return 0
    lax.fori_loop(0, groups, forward, 0)
    def mix(q, _):
        row = pl.ds(q, 96, stride=24)
        s = jnp.concatenate([jnp.concatenate([f_ref[3*part+k, row, :].astype(jnp.bfloat16) for k in range(3)], axis=1) for part in range(2)], axis=0)
        hid = jnp.maximum(dot(w1_ref[...], s) + b1_ref[...], 0.0).astype(jnp.bfloat16)
        out = dot(w2_ref[...], hid)
        out = jnp.where(out > 0.01, out - 0.01, jnp.where(out < -0.01, out + 0.01, 0.0))
        for part in range(2):
            for k in range(3):
                h_ref[3*part+k, row, :] = out[96*part:96*part+96, 128*k:128*k+128]
        return 0
    lax.fori_loop(0, 24, mix, 0)
    def inverse(g, _):
        row = pl.ds(pl.multiple_of(g*384, 384), 384)
        hb = jnp.concatenate([h_ref[k, row, :].astype(jnp.bfloat16) for k in range(6)], axis=1)
        out = dot(ti_ref[...], hb, ((1,),(1,)))
        o_ref[:, :, row] = out.astype(jnp.bfloat16).reshape(16, 48, 384)
        return 0
    lax.fori_loop(0, groups, inverse, 0)

def spectral(r, w1, b1, w2, tf, ti):
    vm = pl.BlockSpec(memory_space=pltpu.VMEM)
    return pl.pallas_call(spectral_kernel, out_shape=jax.ShapeDtypeStruct((16,48,2304), jnp.bfloat16),
        in_specs=[vm]*6, out_specs=vm,
        scratch_shapes=[pltpu.VMEM((768,384), jnp.bfloat16), pltpu.VMEM((6,2304,128), jnp.float32), pltpu.VMEM((6,2304,128), jnp.float32)],
        compiler_params=pltpu.CompilerParams(vmem_limit_bytes=60<<20),
        cost_estimate=pl.CostEstimate(flops=12*10**9, bytes_accessed=10**7, transcendentals=0), name="spectral")(r, w1, b1, w2, tf, ti)

def spatial_kernel(scale_ref, y_ref, v_ref, n_ref, area_ref, tl_ref, u_ref, sum_ref, sq_ref, z_ref):
    g = pl.program_id(0)
    mask = jnp.where(lax.broadcasted_iota(jnp.int32, (1, 384), 1) == 0, 1.0, 2.0)
    for t in range(3):
        xs = [y_ref[p, 16*t:16*t+16, :] for p in range(16)]
        def put(c, v, t=t):
            z_ref[48*c+16*t:48*c+16*t+16, :] = v.astype(jnp.float32) * mask
        exchange_into(xs, 24, put)
    z = z_ref[...].reshape(16, 48, 384)
    lhs = jnp.concatenate([z[:, :24], z[:, 24:]], axis=2).reshape(384, 768).astype(jnp.bfloat16)
    sp = dot(lhs, tl_ref[...]).reshape(16, 24, 768)
    u = sp + n_ref[...].astype(jnp.float32) + v_ref[...].astype(jnp.float32) * scale_ref[0]
    u_ref[...] = u.astype(jnp.bfloat16)
    @pl.when(g == 0)
    def _():
        sum_ref[...] = jnp.zeros_like(sum_ref)
        sq_ref[...] = jnp.zeros_like(sq_ref)
    sum_ref[...] += jnp.sum(u, axis=0)
    sq_ref[...] += jnp.sum(u * u, axis=0)

def spatial(scale, y, v, n, tl):
    vm = pl.BlockSpec(memory_space=pltpu.VMEM)
    blk = pl.BlockSpec((16,24,768), lambda g: (g,0,0))
    acc = pl.BlockSpec((24,768), lambda g: (0,0))
    return pl.pallas_call(lambda s,y,v,n,t,u,a,b,z: spatial_kernel(s,y,v,n,None,t,u,a,b,z),
        out_shape=(jax.ShapeDtypeStruct((96,24,768), jnp.bfloat16), jax.ShapeDtypeStruct((24,768), jnp.float32), jax.ShapeDtypeStruct((24,768), jnp.float32)),
        grid=(6,),
        in_specs=[pl.BlockSpec(memory_space=pltpu.SMEM), pl.BlockSpec((16,48,384), lambda g: (0,0,g)), blk, blk, pl.BlockSpec((768,768), lambda g: (0,0))],
        out_specs=(blk, acc, acc),
        scratch_shapes=[pltpu.VMEM((768,384), jnp.float32)],
        compiler_params=pltpu.CompilerParams(vmem_limit_bytes=50<<20),
        cost_estimate=pl.CostEstimate(flops=3*10**9, bytes_accessed=15*10**6, transcendentals=0), name="spatial")(scale, y, v, n, tl)


def sum_over(x, axes):
    copies = jnp.broadcast_to(x, (lax.axis_size(axes), *x.shape))
    everything = lax.all_to_all(copies, axes, split_axis=0, concat_axis=0, tiled=True)
    return jnp.sum(everything.astype(jnp.float32), axis=0)


def swap_pieces(x):
    return lax.all_to_all(x, LAT, split_axis=0, concat_axis=0, tiled=True)


def complex_weight(w):
    re, im = w[0].T, w[1].T
    return jnp.concatenate([jnp.concatenate([re, -im], 1), jnp.concatenate([im, re], 1)], 0)


def per_device(field_in, ln_gain, ln_shift, mix_first, mix_bias, mix_second):
    ch_dev, band_rows, lon_cells = field_in.shape
    lat_parts = lax.axis_size(LAT)
    lat_rows = band_rows * lat_parts
    ch_all = ch_dev * lax.axis_size(CH)
    tf, ti, tl = (jnp.asarray(t) for t in host_tables())
    t_forward = tl.reshape(2, lat_parts, 24, lon_cells).transpose(1, 0, 2, 3).reshape(768, lon_cells)
    row_pos = (lax.axis_index(LAT) * band_rows + jnp.arange(band_rows)).astype(jnp.float32)
    area = jnp.cos((row_pos + 0.5) * (math.pi / lat_rows) - 0.5 * math.pi)[:, None]
    source = field_in.astype(jnp.float32)
    sums, squares = jnp.sum(source, axis=0), jnp.sum(source * source, axis=0)
    current, scale = field_in, jnp.float32(1.0)
    target_band = target = None
    for layer in range(mix_first.shape[0]):
        stats = sum_over(jnp.stack([sums, squares]).astype(jnp.bfloat16), CH)
        band = jnp.sum(area * stats[1])
        if layer == 0:
            target_band = band
        else:
            both = jnp.broadcast_to(jnp.stack([target_band, band])[:, None], (2, 128))
            both = sum_over(both, LAT)
            target = both[0, 0]
            scale = jnp.sqrt(target / both[1, 0])
        mean = stats[0] / ch_all
        spread = stats[1] / ch_all - mean * mean
        inv_std = scale * lax.rsqrt(spread * (scale * scale) + NORM_EPS)
        gain, shift = ln_gain[layer][:, None, None], ln_shift[layer][:, None, None]
        normed = ((current.astype(jnp.float32) - mean) * inv_std * gain + shift).astype(jnp.bfloat16)
        lon = dot(t_forward, normed.reshape(ch_dev * band_rows, lon_cells), ((1,), (1,)))
        pieces = swap_pieces(lon.astype(jnp.bfloat16).reshape(lat_parts, 48, ch_dev * band_rows))
        bias = mix_bias[layer, :, 0].astype(jnp.float32).reshape(2 * ch_dev, 1)
        back = spectral(
            pieces,
            complex_weight(mix_first[layer, :, 0]),
            bias,
            complex_weight(mix_second[layer, :, 0]),
            tf,
            ti,
        )
        current, sums, squares = spatial(scale.reshape(1), swap_pieces(back), current, normed, tl)
    energy = sum_over(jnp.broadcast_to(jnp.sum(area * squares), (1, 128)), LAT_CH)[0, 0]
    return (current.astype(jnp.float32) * jnp.sqrt(target / energy)).astype(jnp.bfloat16)


def solution(mesh):
    finer = Mesh(mesh.devices.reshape(4, 4, 4, 2), LAT_CH)
    in_specs = (
        P(CH, LAT, None),
        P(None, CH),
        P(None, CH),
        P(None, None, CH, None, None),
        P(None, None, CH, None),
        P(None, None, CH, None, None),
    )
    return jax.shard_map(
        per_device, mesh=finer, in_specs=in_specs, out_specs=P(CH, LAT, None), check_vma=False
    )
```

time: 633 us -> 379 us (0.60)
  matrix products: 124 us -> 8.85 us
  Pallas kernels: 0 us -> 83.4 us
  blocking collectives: 203 us -> 124 us
  local copies, waits for them, and re-layouts: 78.5 us -> 16.9 us
  waiting for transfers between devices: 140 us -> 90 us
  other arithmetic: 45.1 us -> 23.5 us
    dot_general x28 -> x2, matrix products: 124 us -> 8.85 us  [dot(): lax.dot_general(a, b, (dims, ((), ())), preferred_element_type=jnp.float32)]
    pallas_call x0 -> x4, Pallas kernels: none -> 83.4 us  [the longest x2 60.3 us: spectral(): pl.pallas_call(spectral_kernel, out_shape=jax.ShapeDtypeStruct((16, 48, 2...]
    psum x8 -> x0, blocking collectives: 75.4 us -> none  [by_axis(): return functools.reduce(lax.psum, axes, x)]
    all_to_all x5 -> x4, waiting for transfers between devices: 140 us -> 90 us  [the longest x2 70.6 us: swap_pieces(): return lax.all_to_all(x, LAT, split_axis=0, concat_axis=0, tiled=True)]
    all_to_all x6 -> x0, local copies, waits for them, and re-layouts: 31.7 us -> none  [the longest x4 22.5 us: per_device(): lax.all_to_all(lon_spec.reshape(ch_dev, band_rows, lon_cells), LAT, split...]
    another operation x10 -> x5, other arithmetic: 17.8 us -> 2.14 us  [the longest x1 1.32 us: per_device(): both = jnp.broadcast_to(jnp.stack([target_band, band])[:, None], (2, 128))]
    dot_general x2 -> x0, local copies, waits for them, and re-layouts: 13.7 us -> none  [per_device(): jnp.dot(band_spec.reshape(ch_dev * band_rows, lon_cells), inverse, prefer...]
    reshape x2 -> x0, local copies, waits for them, and re-layouts: 12.2 us -> none  [per_device(): lon_spec.reshape(ch_dev, band_rows, lon_cells)]
  transfers between devices with their start and end apart: 5 -> 4, of which waited for: 5 -> 4; matrix products, arithmetic and copies ran while one was open for 1% -> 4% of each run, Pallas kernels for 0% -> 0%
where the time goes in v1:
time: 379 us; the launch traced here: 377 us
  blocking collectives  124 us (33%)
  waiting for transfers between devices  90 us (24%)
  Pallas kernels  83.4 us (22%)
  starting transfers between devices  28.3 us (7%)
  other arithmetic  23.5 us (6%)
  local copies, waits for them, and re-layouts  16.9 us (4%)
  matrix products  8.85 us (2%)
    all_to_all x2, blocking collectives, swap_pieces(): return lax.all_to_all(x, LAT, split_axis=0, concat_axis=0, tiled=True)  94.7 us
    all_to_all x2, waiting for transfers between devices, swap_pieces(): return lax.all_to_all(x, LAT, split_axis=0, concat_axis=0, tiled=True)  70.6 us
    pallas_call x2, Pallas kernels, spectral(): pl.pallas_call(spectral_kernel, out_shape=jax.ShapeDtypeStruct((16, 48, 2...  60.3 us
    all_to_all x2, blocking collectives, sum_over(): lax.all_to_all(copies, axes, split_axis=0, concat_axis=0, tiled=True)  29.4 us
    pallas_call x2, Pallas kernels, spatial(): pl.pallas_call(lambda s, y, v, n, t, u, a, b, z: spatial_kernel(s, y, v,...  23.1 us
    all_to_all x2, waiting for transfers between devices, sum_over(): lax.all_to_all(copies, axes, split_axis=0, concat_axis=0, tiled=True)  19.4 us
    all_to_all x2, starting transfers between devices, sum_over(): lax.all_to_all(copies, axes, split_axis=0, concat_axis=0, tiled=True)  15.8 us
    all_to_all x2, starting transfers between devices, swap_pieces(): return lax.all_to_all(x, LAT, split_axis=0, concat_axis=0, tiled=True)  12.4 us
  transfers between devices with their start and end apart: 4, of which 4 were waited for; matrix products, arithmetic and copies ran while one was open for 4% of the time, Pallas kernels for 0%

profile of v1, /device:TPU:1, one launch (start us, length us, event | category | flops | bytes accessed | tf_op | source)
XLA Modules:
  0.0 377.4 jit_solution(2049589478388994984)
XLA Ops:
  0.0 3.5 fusion.4
  3.5 1.1 reduce.1
  4.6 0.8 pad_maximum_fusion
  5.4 0.9 broadcast_in_dim.4
  6.3 5.8 %all-to-all-start = ((bf16[8,2,24,768]{3,2,1,0:T(8,128)(2,1)}), bf16[8,2,24,768]{3,2,1,0:T(8,128)(2,1)}, u32[]{:S(2)}, u32[]{:S(2)}) async-start(bf16[8,2,24,768]{3,2,1,0:T(8,128)(2,1)} %broadcast_in_dim.4), calls=%async_computation | async-start | bytes 1179648 | tf_op jit(solution)/shard_map/all_to_all | solution.py:125
  12.1 0.8 slice_bitcast_fusion
  12.9 9.4 %all-to-all-done = bf16[8,2,24,768]{3,2,1,0:T(8,128)(2,1)} async-done(((bf16[8,2,24,768]{3,2,1,0:T(8,128)(2,1)}), bf16[8,2,24,768]{3,2,1,0:T(8,128)(2,1)}, u32[]{:S(2)}, u32[]{:S(2)}) %all-to-all-start) | async-done | bytes 589856 | tf_op jit(solution)/shard_map/all_to_all | solution.py:125
  22.2 1.2 convert_reduce_fusion.1
  23.4 0.6 copy-done.5
  24.1 1.3 fusion.3.n
  25.4 4.4 %convolution_convert_fusion.1 = bf16[2304,768]{0,1:T(8,128)(2,1)} fusion(bf16[2304,768]{1,0:T(8,128)(2,1)S(1)} %bitcast.84, bf16[768,768]{1,0:T(8,128)(2,1)S(1)} %copy-done.11), kind=kOutput, calls=%fused_computation.10 | convolution fusion | flops 2719678464 | bytes 8257536 | tf_op jit(solution)/shard_map/dot_general | solution.py:41
  29.8 7.8 %all-to-all-start.1 = ((bf16[16,48,2304]{2,1,0:T(8,128)(2,1)}), bf16[16,48,2304]{2,1,0:T(8,128)(2,1)S(1)}, u32[]{:S(2)}, u32[]{:S(2)}) async-start(bf16[16,48,2304]{2,1,0:T(8,128)(2,1)} %bitcast.86), calls=%async_computation.1 | async-start | bytes 7077888 | tf_op jit(solution)/shard_map/all_to_all | solution.py:130
  37.6 1.4 fusion.9
  39.0 1.4 copy.54
  40.5 1.4 fusion.10
  41.9 1.4 copy.52
  43.3 1.4 copy.51
  44.8 1.4 copy.53
  46.2 0.7 slice_convert_fusion
  46.9 0.8 reshape.91.b1_ref
  47.7 0.7 bitcast_negate_fusion.2
  48.4 0.7 bitcast_negate_fusion.3
  49.2 1.7 maximum_maximum_fusion
  50.8 31.3 %all-to-all-done.1.r_ref = bf16[16,48,2304]{2,1,0:T(8,128)(2,1)S(1)} async-done(((bf16[16,48,2304]{2,1,0:T(8,128)(2,1)}), bf16[16,48,2304]{2,1,0:T(8,128)(2,1)S(1)}, u32[]{:S(2)}, u32[]{:S(2)}) %all-to-all-start.1) | async-done | bytes 3538976 | tf_op jit(solution)/shard_map/all_to_all | solution.py:130
  82.1 1.8 copy-done.4
  83.9 30.1 %spectral.2 = bf16[16,48,2304]{2,1,0:T(8,128)(2,1)} custom-call(bf16[16,48,2304]{2,1,0:T(8,128)(2,1)} %copy-done.4, bf16[192,192]{1,0:T(8,128)(2,1)} %get-tuple-element.39.w1_ref, f32[192,1]{1,0:T(8,128)} %reshape.91.b1_ref, bf16[192,192]{1,0:T(8,128)(2,1)} %get-tuple-element.40.w2_ref, bf16[384,768]{1,0:T(8,128)(2,1)} %constant.38.clone.tf_ref, ...), custom_call_target="tpu_custom_call" | custom-call | flops 12000000000 | bytes 10000000 | tf_op jit(solution)/shard_map/spectral/pallas_call | solution.py:83
  114.1 50.0 %all_to_all.40.y = bf16[16,48,2304]{2,1,0:T(8,128)(2,1)} all-to-all(bf16[16,48,2304]{2,1,0:T(8,128)(2,1)} %spectral.2), channel_id=1, replica_groups=mesh['lat_0'=4,'lat_1'=4,'ch_0'=4,'ch_1'=2] {'lat_0','lat_1'}, dimensions={0} | all-to-all | bytes 7077888 | tf_op jit(solution)/shard_map/all_to_all | solution.py:130
  164.0 11.6 %spatial.2 = (bf16[96,24,768]{2,1,0:T(8,128)(2,1)}, f32[24,768]{1,0:T(8,128)S(1)}, f32[24,768]{1,0:T(8,128)S(1)}) custom-call(f32[1]{0:T(128)} %constant.35.clone.1.s, bf16[16,48,2304]{2,1,0:T(8,128)(2,1)} %all_to_all.40.y, bf16[96,24,768]{2,1,0:T(8,128)(2,1)} %v.1, bf16[96,24,768]{2,1,0:T(8,128)(2,1)} %copy-done.2, bf16[768,768]{1,0:T(8,128)(2,1)S(1)} %copy-done), custom_call_target="tpu_custom_call" | custom-call | flops 3000000000 | bytes 15000000 | tf_op jit(solution)/shard_map/spatial/pallas_call | solution.py:113
  175.7 0.9 broadcast_in_dim.5
  176.5 10.1 %all-to-all-start.3 = ((bf16[8,2,24,768]{3,2,1,0:T(8,128)(2,1)}), bf16[8,2,24,768]{3,2,1,0:T(8,128)(2,1)S(1)}, u32[]{:S(2)}, u32[]{:S(2)}) async-start(bf16[8,2,24,768]{3,2,1,0:T(8,128)(2,1)} %broadcast_in_dim.5), calls=%async_computation.3 | async-start | bytes 1179648 | tf_op jit(solution)/shard_map/all_to_all | solution.py:125
  186.6 10.0 %all-to-all-done.3 = bf16[8,2,24,768]{3,2,1,0:T(8,128)(2,1)S(1)} async-done(((bf16[8,2,24,768]{3,2,1,0:T(8,128)(2,1)}), bf16[8,2,24,768]{3,2,1,0:T(8,128)(2,1)S(1)}, u32[]{:S(2)}, u32[]{:S(2)}) %all-to-all-start.3) | async-done | bytes 589856 | tf_op jit(solution)/shard_map/all_to_all | solution.py:125
  196.7 0.8 fusion.6
  197.5 1.3 pad_maximum_fusion.2
  198.9 9.7 %all_to_all.41 = f32[16,2,128]{2,1,0:T(2,128)S(1)} all-to-all(f32[16,2,128]{2,1,0:T(2,128)S(1)} %broadcast_in_dim_broadcast_in_dim.8), channel_id=1, replica_groups=mesh['lat_0'=4,'lat_1'=4,'ch_0'=4,'ch_1'=2] {'lat_0','lat_1'}, dimensions={0} | all-to-all | bytes 32768 | tf_op jit(solution)/shard_map/all_to_all | solution.py:125
  208.6 0.6 fusion.11
  210.6 3.4 add_convert_fusion.n
  214.0 4.5 %convolution_convert_fusion = bf16[2304,768]{0,1:T(8,128)(2,1)} fusion(bf16[2304,768]{1,0:T(8,128)(2,1)S(1)} %bitcast.85, bf16[768,768]{1,0:T(8,128)(2,1)S(1)} %copy-done.12), kind=kOutput, calls=%fused_computation.9 | convolution fusion | flops 2719678464 | bytes 8257536 | tf_op jit(solution)/shard_map/dot_general | solution.py:41
  218.5 4.7 %all-to-all-start.5 = ((bf16[16,48,2304]{2,1,0:T(8,128)(2,1)}), bf16[16,48,2304]{2,1,0:T(8,128)(2,1)}, u32[]{:S(2)}, u32[]{:S(2)}) async-start(bf16[16,48,2304]{2,1,0:T(8,128)(2,1)} %bitcast.87), calls=%async_computation.5 | async-start | bytes 7077888 | tf_op jit(solution)/shard_map/all_to_all | solution.py:130
  223.6 0.8 reshape.92.b1_ref
  224.5 0.8 maximum_maximum_fusion.2
  225.3 39.3 %all-to-all-done.5.r_ref = bf16[16,48,2304]{2,1,0:T(8,128)(2,1)} async-done(((bf16[16,48,2304]{2,1,0:T(8,128)(2,1)}), bf16[16,48,2304]{2,1,0:T(8,128)(2,1)}, u32[]{:S(2)}, u32[]{:S(2)}) %all-to-all-start.5) | async-done | bytes 3538976 | tf_op jit(solution)/shard_map/all_to_all | solution.py:130
  264.6 30.2 %spectral.3 = bf16[16,48,2304]{2,1,0:T(8,128)(2,1)} custom-call(bf16[16,48,2304]{2,1,0:T(8,128)(2,1)} %all-to-all-done.5.r_ref, bf16[192,192]{1,0:T(8,128)(2,1)} %get-tuple-element.41.w1_ref, f32[192,1]{1,0:T(8,128)} %reshape.92.b1_ref, bf16[192,192]{1,0:T(8,128)(2,1)} %get-tuple-element.42.w2_ref, bf16[384,768]{1,0:T(8,128)(2,1)} %constant.38.clone.tf_ref, ...), custom_call_target="tpu_custom_call" | custom-call | flops 12000000000 | bytes 10000000 | tf_op jit(solution)/shard_map/spectral/pallas_call | solution.py:83
  294.8 44.8 %all_to_all.42.y = bf16[16,48,2304]{2,1,0:T(8,128)(2,1)} all-to-all(bf16[16,48,2304]{2,1,0:T(8,128)(2,1)} %spectral.3), channel_id=1, replica_groups=mesh['lat_0'=4,'lat_1'=4,'ch_0'=4,'ch_1'=2] {'lat_0','lat_1'}, dimensions={0} | all-to-all | bytes 7077888 | tf_op jit(solution)/shard_map/all_to_all | solution.py:130
  339.6 11.6 %spatial.3 = (bf16[96,24,768]{2,1,0:T(8,128)(2,1)}, f32[24,768]{1,0:T(8,128)}, f32[24,768]{1,0:T(8,128)S(1)}) custom-call(f32[1]{0:T(128)} %bitcast.27.s, bf16[16,48,2304]{2,1,0:T(8,128)(2,1)} %all_to_all.42.y, bf16[96,24,768]{2,1,0:T(8,128)(2,1)} %get-tuple-element.12.v, bf16[96,24,768]{2,1,0:T(8,128)(2,1)} %copy-done.3, bf16[768,768]{1,0:T(8,128)(2,1)S(1)} %copy-done), custom_call_target="tpu_custom_call" | custom-call | flops 3000000000 | bytes 15000000 | tf_op jit(solution)/shard_map/spatial/pallas_call | solution.py:113
  351.1 0.7 multiply_reduce_fusion
  351.8 0.7 broadcast_in_dim_broadcast_in_dim.9
  352.5 19.6 %all_to_all.43 = f32[128,1,128]{2,1,0:T(1,128)S(1)} all-to-all(f32[128,1,128]{2,1,0:T(1,128)S(1)} %broadcast_in_dim_broadcast_in_dim.9), channel_id=1, replica_groups=mesh['lat_0'=4,'lat_1'=4,'ch_0'=4,'ch_1'=2] {'lat_0','lat_1','ch_0','ch_1'}, dimensions={0} | all-to-all | bytes 131072 | tf_op jit(solution)/shard_map/all_to_all | solution.py:125
  372.9 4.5 %multiply_convert_fusion = bf16[96,24,768]{2,1,0:T(8,128)(2,1)} fusion(bf16[96,24,768]{2,1,0:T(8,128)(2,1)} %get-tuple-element.13, f32[]{:T(128)} %bitcast.50), kind=kLoop, calls=%fused_computation.7 | loop fusion | flops 5308416 | bytes 7077892 | tf_op jit(solution)/shard_map/convert_element_type | solution.py:179
  (40 shorter events, 0.8 us)
Async XLA Ops:
  0.0 3.5 copy-start.1
  6.3 15.9 %all-to-all-start = ((bf16[8,2,24,768]{3,2,1,0:T(8,128)(2,1)}), bf16[8,2,24,768]{3,2,1,0:T(8,128)(2,1)}, u32[]{:S(2)}, u32[]{:S(2)}) async-start(bf16[8,2,24,768]{3,2,1,0:T(8,128)(2,1)} %broadcast_in_dim.4), calls=%async_computation | async-start | bytes 1179648 | tf_op jit(solution)/shard_map/all_to_all | solution.py:125
  23.4 0.7 copy-start.5
  24.1 1.3 copy-start.11
  25.4 4.4 %copy-start.2 = (bf16[96,24,768]{2,1,0:T(8,128)(2,1)}, bf16[96,24,768]{2,1,0:T(8,128)(2,1)S(1)}, u32[]{:S(2)}) copy-start(bf16[96,24,768]{2,1,0:T(8,128)(2,1)S(1)} %fusion.3.n) | copy-start | bytes 10616836
  29.8 52.3 %all-to-all-start.1 = ((bf16[16,48,2304]{2,1,0:T(8,128)(2,1)}), bf16[16,48,2304]{2,1,0:T(8,128)(2,1)S(1)}, u32[]{:S(2)}, u32[]{:S(2)}) async-start(bf16[16,48,2304]{2,1,0:T(8,128)(2,1)} %bitcast.86), calls=%async_computation.1 | async-start | bytes 7077888 | tf_op jit(solution)/shard_map/all_to_all | solution.py:130
  82.1 1.8 copy-start.4
  114.1 50.0 %copy-start = (bf16[768,768]{1,0:T(8,128)(2,1)S(1)}, bf16[768,768]{1,0:T(8,128)(2,1)}, u32[]{:S(2)}) copy-start(bf16[768,768]{1,0:T(8,128)(2,1)} %constant.40.clone.t) | copy-start | bytes 3538948
  164.0 32.7 %copy-start.6 = (f32[2,24,768]{2,1,0:T(8,128)S(1)}, f32[2,24,768]{2,1,0:T(8,128)}, u32[]{:S(2)}) copy-start(f32[2,24,768]{2,1,0:T(8,128)} %copy-done.5) | copy-start | bytes 442372
  176.5 20.1 %all-to-all-start.3 = ((bf16[8,2,24,768]{3,2,1,0:T(8,128)(2,1)}), bf16[8,2,24,768]{3,2,1,0:T(8,128)(2,1)S(1)}, u32[]{:S(2)}, u32[]{:S(2)}) async-start(bf16[8,2,24,768]{3,2,1,0:T(8,128)(2,1)} %broadcast_in_dim.5), calls=%async_computation.3 | async-start | bytes 1179648 | tf_op jit(solution)/shard_map/all_to_all | solution.py:125
  210.6 3.4 copy-start.12
  214.0 4.5 %copy-start.3 = (bf16[96,24,768]{2,1,0:T(8,128)(2,1)}, bf16[96,24,768]{2,1,0:T(8,128)(2,1)S(1)}, u32[]{:S(2)}) copy-start(bf16[96,24,768]{2,1,0:T(8,128)(2,1)S(1)} %add_convert_fusion.n) | copy-start | bytes 10616836
  218.5 4.7 %copy-start.8 = (bf16[1,1,1,96,96]{4,3,2,1,0:T(8,128)(2,1)S(1)}, bf16[1,1,1,96,96]{4,3,2,1,0:T(8,128)(2,1)}, u32[]{:S(2)}) copy-start(bf16[1,1,1,96,96]{4,3,2,1,0:T(8,128)(2,1)} %get-tuple-element.21) | copy-start | bytes 55300
  218.5 4.8 %copy-start.10 = (bf16[1,1,1,96,96]{4,3,2,1,0:T(8,128)(2,1)S(1)}, bf16[1,1,1,96,96]{4,3,2,1,0:T(8,128)(2,1)}, u32[]{:S(2)}) copy-start(bf16[1,1,1,96,96]{4,3,2,1,0:T(8,128)(2,1)} %get-tuple-element.25) | copy-start | bytes 55300
  218.5 4.9 %copy-start.9 = (bf16[1,1,1,96,96]{4,3,2,1,0:T(8,128)(2,1)S(1)}, bf16[1,1,1,96,96]{4,3,2,1,0:T(8,128)(2,1)}, u32[]{:S(2)}) copy-start(bf16[1,1,1,96,96]{4,3,2,1,0:T(8,128)(2,1)} %get-tuple-element.26) | copy-start | bytes 55300
  218.5 5.0 %copy-start.7 = (bf16[1,1,1,96,96]{4,3,2,1,0:T(8,128)(2,1)S(1)}, bf16[1,1,1,96,96]{4,3,2,1,0:T(8,128)(2,1)}, u32[]{:S(2)}) copy-start(bf16[1,1,1,96,96]{4,3,2,1,0:T(8,128)(2,1)} %get-tuple-element.22) | copy-start | bytes 55300
  218.5 46.1 %all-to-all-start.5 = ((bf16[16,48,2304]{2,1,0:T(8,128)(2,1)}), bf16[16,48,2304]{2,1,0:T(8,128)(2,1)}, u32[]{:S(2)}, u32[]{:S(2)}) async-start(bf16[16,48,2304]{2,1,0:T(8,128)(2,1)} %bitcast.87), calls=%async_computation.5 | async-start | bytes 7077888 | tf_op jit(solution)/shard_map/all_to_all | solution.py:130

commit v2 on v1

v2 whole, which is shorter than its diff:
```python
import functools
import math

import jax
import jax.numpy as jnp
import numpy as np
from jax import lax
from jax.experimental import pallas as pl
from jax.experimental.pallas import tpu as pltpu
from jax.sharding import Mesh
from jax.sharding import PartitionSpec as P

CH = ("ch_0", "ch_1")
LAT = ("lat_0", "lat_1")
LAT_CH = LAT + CH
NORM_EPS = 1e-05


def host_tables():
    def trig(length, freqs):
        n = np.arange(length)
        a = (n[:, None] * freqs[None, :] % length) * (2.0*math.pi/length)
        s = 1.0/math.sqrt(length)
        bf = jnp.bfloat16
        return (np.cos(a)*s).astype(bf), (np.sin(a)*s).astype(bf)
    c, s = trig(384, np.arange(384))
    tf = np.concatenate([c, s], 1)
    re = np.concatenate([c.T, -s.T], 1).reshape(16, 24, 768)
    im = np.concatenate([s.T, c.T], 1).reshape(16, 24, 768)
    ti = np.stack([re, im], 1).reshape(768, 768)
    lc, ls = trig(768, np.arange(384))
    t = np.concatenate([lc.T, -ls.T], 0)
    return tf, ti, t


MIX_STEP = 8
SPECTRAL_VMEM = 36 << 20
SPATIAL_VMEM = 28 << 20
NORM_VMEM = 24 << 20


def exchange_into(xs, unit, put):
    for c in range(len(xs)):
        put(c, jnp.concatenate([x[:, unit*c:unit*(c+1)] for x in xs], axis=1))

def dot(a, b, dims=((1,),(0,))):
    return lax.dot_general(a, b, (dims, ((),())), preferred_element_type=jnp.float32)

def complex_weight(w_ref):
    re, im = (w_ref[part, 0].astype(jnp.float32).T for part in range(2))
    rows = [jnp.concatenate([re, -im], axis=1), jnp.concatenate([im, re], axis=1)]
    return jnp.concatenate(rows, axis=0).astype(jnp.bfloat16)


def spectral_kernel(r_ref, wa_ref, ba_ref, wb_ref, tf_hbm, ti_hbm, o_ref, g_ref, f_ref, h_ref, tf_ref, ti_ref, sems):
    load_tf = pltpu.make_async_copy(tf_hbm, tf_ref, sems.at[0])
    load_ti = pltpu.make_async_copy(ti_hbm, ti_ref, sems.at[1])
    load_tf.start()
    load_ti.start()
    w1, w2 = complex_weight(wa_ref), complex_weight(wb_ref)
    b1 = jnp.concatenate([ba_ref[part].astype(jnp.float32).reshape(1, -1).T for part in range(2)], axis=0)
    load_tf.wait()
    groups = r_ref.shape[2] // 384

    def forward(g, _):
        l = pl.ds(pl.multiple_of(g * 384, 384), 384)
        for t in range(3):
            def put(c, v, t=t):
                g_ref[48 * c + 16 * t : 48 * c + 16 * t + 16, :] = v

            exchange_into([r_ref[p, 16 * t : 16 * t + 16, l] for p in range(16)], 24, put)
        prod = dot(g_ref[...], tf_ref[...]).reshape(16, 48, 768)
        re, im = prod[:, :24], prod[:, 24:]
        for k in range(3):
            a, b = slice(128 * k, 128 * k + 128), slice(384 + 128 * k, 512 + 128 * k)
            f_ref[k, l, :] = (re[:, :, a] + im[:, :, b]).reshape(384, 128)
            f_ref[3 + k, l, :] = (im[:, :, a] - re[:, :, b]).reshape(384, 128)
        return 0

    def mix(i, _):
        rows = [pl.ds(i * MIX_STEP + k, 96, stride=24) for k in range(MIX_STEP)]
        s = jnp.concatenate(
            [
                jnp.concatenate(
                    [f_ref[3 * part + k, row, :].astype(jnp.bfloat16) for row in rows for k in range(3)], axis=1
                )
                for part in range(2)
            ],
            axis=0,
        )
        hid = jnp.maximum(dot(w1, s) + b1, 0.0).astype(jnp.bfloat16)
        out = dot(w2, hid)
        out = jnp.where(out > 0.01, out - 0.01, jnp.where(out < -0.01, out + 0.01, 0.0))
        for n, row in enumerate(rows):
            for part in range(2):
                for k in range(3):
                    lane = 384 * n + 128 * k
                    h_ref[3 * part + k, row, :] = out[96 * part : 96 * part + 96, lane : lane + 128]
        return 0

    def inverse(g, _):
        row = pl.ds(pl.multiple_of(g * 384, 384), 384)
        hb = jnp.concatenate([h_ref[k, row, :].astype(jnp.bfloat16) for k in range(6)], axis=1)
        out = dot(ti_ref[...], hb, ((1,), (1,)))
        o_ref[:, :, row] = out.astype(jnp.bfloat16).reshape(16, 48, 384)
        return 0

    lax.fori_loop(0, groups, forward, 0, unroll=3)
    lax.fori_loop(0, 24 // MIX_STEP, mix, 0)
    load_ti.wait()
    lax.fori_loop(0, groups, inverse, 0, unroll=2)


def spectral(r, wa, ba, wb, tf, ti):
    vm, hbm = pl.BlockSpec(memory_space=pltpu.VMEM), pl.BlockSpec(memory_space=pltpu.HBM)
    return pl.pallas_call(
        spectral_kernel,
        out_shape=jax.ShapeDtypeStruct(r.shape, jnp.bfloat16),
        in_specs=[vm] * 4 + [hbm] * 2,
        out_specs=vm,
        scratch_shapes=[
            pltpu.VMEM((768, 384), jnp.bfloat16),
            pltpu.VMEM((6, 2304, 128), jnp.float32),
            pltpu.VMEM((6, 2304, 128), jnp.float32),
            pltpu.VMEM(tf.shape, tf.dtype),
            pltpu.VMEM(ti.shape, ti.dtype),
            pltpu.SemaphoreType.DMA((2,)),
        ],
        compiler_params=pltpu.CompilerParams(vmem_limit_bytes=SPECTRAL_VMEM),
        cost_estimate=pl.CostEstimate(flops=12 * 10**9, bytes_accessed=10**7, transcendentals=0),
        name="spectral",
    )(r, wa, ba, wb, tf, ti)


def spatial_kernel(last, scale_ref, y_ref, v_ref, n_ref, tl_ref, u_ref, st_ref, z_ref, sum_ref, sq_ref):
    mask = jnp.where(lax.broadcasted_iota(jnp.int32, (1, 384), 1) == 0, 1.0, 2.0)
    sum_ref[...] = jnp.zeros_like(sum_ref)
    sq_ref[...] = jnp.zeros_like(sq_ref)

    def inverse(g, _):
        l = pl.ds(pl.multiple_of(g * 384, 384), 384)
        for t in range(3):
            def put(c, v, t=t):
                z_ref[48 * c + 16 * t : 48 * c + 16 * t + 16, :] = v.astype(jnp.float32) * mask

            exchange_into([y_ref[p, 16 * t : 16 * t + 16, l] for p in range(16)], 24, put)
        z = z_ref[...].reshape(16, 48, 384)
        lhs = jnp.concatenate([z[:, :24], z[:, 24:]], axis=2).reshape(384, 768).astype(jnp.bfloat16)
        sp = dot(lhs, tl_ref[...]).reshape(16, 24, 768)
        d = pl.ds(pl.multiple_of(g * 16, 16), 16)
        u = sp + n_ref[d].astype(jnp.float32) + v_ref[d].astype(jnp.float32) * scale_ref[0]
        u_ref[d] = u.astype(jnp.bfloat16)
        sum_ref[...] += jnp.sum(u, axis=0)
        sq_ref[...] += jnp.sum(u * u, axis=0)
        return 0

    lax.fori_loop(0, 6, inverse, 0, unroll=2)
    if last:
        st_ref[...] = sq_ref[...]
    else:
        put_stats(st_ref, sum_ref[...], sq_ref[...])


def put_stats(st_ref, sums, squares):
    for dest in range(st_ref.shape[0]):
        st_ref[dest, 0] = sums.astype(jnp.bfloat16)
        st_ref[dest, 1] = squares.astype(jnp.bfloat16)


def spatial(scale, y, v, n, tl, last):
    vm = pl.BlockSpec(memory_space=pltpu.VMEM)
    plane = v.shape[1:]
    stats = jax.ShapeDtypeStruct(plane, jnp.float32) if last else jax.ShapeDtypeStruct((8, 2, *plane), jnp.bfloat16)

    def body(*refs):
        spatial_kernel(last, *refs)

    return pl.pallas_call(
        body,
        out_shape=(jax.ShapeDtypeStruct(v.shape, jnp.bfloat16), stats),
        in_specs=[pl.BlockSpec(memory_space=pltpu.SMEM)] + [vm] * 4,
        out_specs=(vm, vm),
        scratch_shapes=[pltpu.VMEM((768, 384), jnp.float32), pltpu.VMEM(plane, jnp.float32), pltpu.VMEM(plane, jnp.float32)],
        compiler_params=pltpu.CompilerParams(vmem_limit_bytes=SPATIAL_VMEM),
        cost_estimate=pl.CostEstimate(flops=3 * 10**9, bytes_accessed=15 * 10**6, transcendentals=0),
        name="spatial",
    )(scale, y, v, n, tl)


def stats_kernel(v_ref, st_ref, sum_ref, sq_ref):
    g = pl.program_id(0)

    @pl.when(g == 0)
    def _():
        sum_ref[...] = jnp.zeros_like(sum_ref)
        sq_ref[...] = jnp.zeros_like(sq_ref)

    v = v_ref[...].astype(jnp.float32)
    sum_ref[...] += jnp.sum(v, axis=0)
    sq_ref[...] += jnp.sum(v * v, axis=0)

    @pl.when(g == pl.num_programs(0) - 1)
    def _():
        put_stats(st_ref, sum_ref[...], sq_ref[...])


def first_stats(v):
    plane = v.shape[1:]
    return pl.pallas_call(
        stats_kernel,
        out_shape=jax.ShapeDtypeStruct((8, 2, *plane), jnp.bfloat16),
        grid=(4,),
        in_specs=[pl.BlockSpec((24, *plane), lambda g: (g, 0, 0))],
        out_specs=pl.BlockSpec((8, 2, *plane), lambda g: (0, 0, 0, 0)),
        scratch_shapes=[pltpu.VMEM(plane, jnp.float32), pltpu.VMEM(plane, jnp.float32)],
        compiler_params=pltpu.CompilerParams(vmem_limit_bytes=16 << 20),
        cost_estimate=pl.CostEstimate(flops=6 * 10**6, bytes_accessed=4 * 10**6, transcendentals=0),
        name="first_stats",
    )(v)


def norm_kernel(scale_ref, gain_ref, shift_ref, v_ref, st_ref, tw_ref, n_ref, o_ref, mean_ref, inv_ref):
    ch_all = 768
    scale = scale_ref[0]
    total, squares = st_ref[0].astype(jnp.float32), st_ref[1].astype(jnp.float32)
    mean = total / ch_all
    spread = squares / ch_all - mean * mean
    mean_ref[...] = mean
    inv_ref[...] = scale * lax.rsqrt(spread * (scale * scale) + NORM_EPS)

    def group(g, _):
        mean, inv = mean_ref[...], inv_ref[...]
        rows = []
        for i in range(16):
            c = g * 16 + i
            normed = (v_ref[c].astype(jnp.float32) - mean) * inv * gain_ref[c] + shift_ref[c]
            rows.append(normed)
        x = jnp.concatenate(rows, axis=0).astype(jnp.bfloat16)
        n_ref[pl.ds(pl.multiple_of(g * 16, 16), 16)] = x.astype(jnp.float32).reshape(16, 24, 768).astype(jnp.bfloat16)
        out = dot(tw_ref[...], x, ((1,), (1,)))
        o_ref[:, :, pl.ds(pl.multiple_of(g * 384, 384), 384)] = out.astype(jnp.bfloat16).reshape(16, 48, 384)
        return 0

    lax.fori_loop(0, 6, group, 0, unroll=2)


def norm_lon(scale, gain, shift, v, stats, tw):
    vm, sm = pl.BlockSpec(memory_space=pltpu.VMEM), pl.BlockSpec(memory_space=pltpu.SMEM)
    plane = v.shape[1:]
    return pl.pallas_call(
        norm_kernel,
        out_shape=(jax.ShapeDtypeStruct(v.shape, jnp.bfloat16), jax.ShapeDtypeStruct((16, 48, 2304), jnp.bfloat16)),
        in_specs=[sm] * 3 + [vm] * 3,
        out_specs=(vm, vm),
        scratch_shapes=[pltpu.VMEM(plane, jnp.float32), pltpu.VMEM(plane, jnp.float32)],
        compiler_params=pltpu.CompilerParams(vmem_limit_bytes=NORM_VMEM),
        cost_estimate=pl.CostEstimate(flops=3 * 10**9, bytes_accessed=10**7, transcendentals=0),
        name="norm_lon",
    )(scale, gain, shift, v, stats, tw)


def final_kernel(scale_ref, u_ref, o_ref):
    d = pl.ds(pl.multiple_of(pl.program_id(0) * o_ref.shape[0], 8), o_ref.shape[0])
    o_ref[...] = (u_ref[d].astype(jnp.float32) * scale_ref[0]).astype(jnp.bfloat16)


def final_scale(scale, u):
    return pl.pallas_call(
        final_kernel,
        out_shape=jax.ShapeDtypeStruct(u.shape, jnp.bfloat16),
        grid=(6,),
        in_specs=[pl.BlockSpec(memory_space=pltpu.SMEM), pl.BlockSpec(memory_space=pltpu.VMEM)],
        out_specs=pl.BlockSpec((16, *u.shape[1:]), lambda g: (g, 0, 0)),
        compiler_params=pltpu.CompilerParams(vmem_limit_bytes=12 << 20),
        cost_estimate=pl.CostEstimate(flops=10**7, bytes_accessed=7 * 10**6, transcendentals=0),
        name="final_scale",
    )(scale, u)


def sum_over(x, axes):
    copies = jnp.broadcast_to(x, (lax.axis_size(axes), *x.shape))
    everything = lax.all_to_all(copies, axes, split_axis=0, concat_axis=0, tiled=True)
    return jnp.sum(everything.astype(jnp.float32), axis=0)


def swap_pieces(x):
    return lax.all_to_all(x, LAT, split_axis=0, concat_axis=0, tiled=True)


def per_device(field_in, ln_gain, ln_shift, mix_first, mix_bias, mix_second):
    ch_dev, band_rows, lon_cells = field_in.shape
    lat_parts = lax.axis_size(LAT)
    lat_rows = band_rows * lat_parts
    tf, ti, tl = (jnp.asarray(t) for t in host_tables())
    t_forward = tl.reshape(2, lat_parts, 24, lon_cells).transpose(1, 0, 2, 3).reshape(768, lon_cells)
    row_pos = (lax.axis_index(LAT) * band_rows + jnp.arange(band_rows)).astype(jnp.float32)
    area = jnp.cos((row_pos + 0.5) * (math.pi / lat_rows) - 0.5 * math.pi)[:, None]
    current, scale = field_in, jnp.float32(1.0)
    stats = first_stats(field_in)
    target_band = target = None
    layers = mix_first.shape[0]
    for layer in range(layers):
        stats = jnp.sum(lax.all_to_all(stats, CH, split_axis=0, concat_axis=0, tiled=True).astype(jnp.float32), axis=0)
        band = jnp.sum(area * stats[1])
        if layer == 0:
            target_band = band
        else:
            both = jnp.broadcast_to(jnp.stack([target_band, band])[:, None], (2, 128))
            both = sum_over(both, LAT)
            target = both[0, 0]
            scale = jnp.sqrt(target / both[1, 0])
        scale_1 = scale.reshape(1)
        normed, lon = norm_lon(scale_1, ln_gain[layer], ln_shift[layer], current, stats, t_forward)
        back = spectral(swap_pieces(lon), mix_first[layer], mix_bias[layer], mix_second[layer], tf, ti)
        current, stats = spatial(scale_1, swap_pieces(back), current, normed, tl, layer == layers - 1)
    energy = sum_over(jnp.broadcast_to(jnp.sum(area * stats), (1, 128)), LAT_CH)[0, 0]
    return final_scale(jnp.sqrt(target / energy).reshape(1), current)


def solution(mesh):
    finer = Mesh(mesh.devices.reshape(4, 4, 4, 2), LAT_CH)
    in_specs = (
        P(CH, LAT, None),
        P(None, CH),
        P(None, CH),
        P(None, None, CH, None, None),
        P(None, None, CH, None),
        P(None, None, CH, None, None),
    )
    return jax.shard_map(
        per_device, mesh=finer, in_specs=in_specs, out_specs=P(CH, LAT, None), check_vma=False
    )
```

time: 379 us -> 356 us (0.939)
  Pallas kernels: 83.4 us -> 62.9 us
  other arithmetic: 23.5 us -> 5.82 us
  waiting for transfers between devices: 90 us -> 104 us
  local copies, waits for them, and re-layouts: 16.9 us -> 28.7 us
  matrix products: 8.85 us -> 0 us
    pallas_call x4 -> x8, Pallas kernels: 83.4 us -> 62.9 us  [the longest x2 34.5 us: spectral(): pl.pallas_call(spectral_kernel, out_shape=jax.ShapeDtypeStruct(r.shape, j...]
    unnamed x34 -> x54, local copies, waits for them, and re-layouts: 8.6 us -> 25 us
    all_to_all x2, waiting for transfers between devices: 70.6 us -> 84.4 us  [swap_pieces(): return lax.all_to_all(x, LAT, split_axis=0, concat_axis=0, tiled=True)]
    convert_element_type x4 -> x0, other arithmetic: 9.9 us -> none  [the longest x2 4.75 us: per_device(): ((current.astype(jnp.float32) - mean) * inv_std * gain + shift).astype(jn...]
    dot_general x2 -> x0, matrix products: 8.85 us -> none  [dot(): lax.dot_general(a, b, (dims, ((), ())), preferred_element_type=jnp.float32)]
  transfers between devices with their start and end apart: 4 -> 4, of which waited for: 4 -> 4; matrix products, arithmetic and copies ran while one was open for 4% -> 1% of each run, Pallas kernels for 0% -> 0%
where the time goes in v2:
time: 356 us; the launch traced here: 355 us
  blocking collectives  124 us (35%)
  waiting for transfers between devices  104 us (29%)
  Pallas kernels  62.9 us (18%)
  local copies, waits for them, and re-layouts  28.7 us (8%)
  starting transfers between devices  27.6 us (8%)
  other arithmetic  5.82 us (2%)
    all_to_all x2, blocking collectives, swap_pieces(): return lax.all_to_all(x, LAT, split_axis=0, concat_axis=0, tiled=True)  95.5 us
    all_to_all x2, waiting for transfers between devices, swap_pieces(): return lax.all_to_all(x, LAT, split_axis=0, concat_axis=0, tiled=True)  84.4 us
    pallas_call x2, Pallas kernels, spectral(): pl.pallas_call(spectral_kernel, out_shape=jax.ShapeDtypeStruct(r.shape, j...  34.5 us
    all_to_all x2, blocking collectives, sum_over(): lax.all_to_all(copies, axes, split_axis=0, concat_axis=0, tiled=True)  28.4 us
    unnamed x54, local copies, waits for them, and re-layouts  25 us
    all_to_all x2, waiting for transfers between devices, per_device(): lax.all_to_all(stats, CH, split_axis=0, concat_axis=0, tiled=True)  19.4 us
    all_to_all x2, starting transfers between devices, per_device(): lax.all_to_all(stats, CH, split_axis=0, concat_axis=0, tiled=True)  15.9 us
    pallas_call x2, Pallas kernels, spatial(): pl.pallas_call(body, out_shape=(jax.ShapeDtypeStruct(v.shape, jnp.bfloat1...  15 us
  transfers between devices with their start and end apart: 4, of which 4 were waited for; matrix products, arithmetic and copies ran while one was open for 1% of the time, Pallas kernels for 0%

profile of v2, /device:TPU:1, one launch (start us, length us, event | category | flops | bytes accessed | tf_op | source)
XLA Modules:
  0.0 355.0 jit_solution(844837662388677326)
XLA Ops:
  0.0 2.0 copy-done
  2.0 0.8 first_stats.1
  2.8 0.8 copy-done.13
  3.6 5.8 %all-to-all-start = ((bf16[8,2,24,768]{3,2,1,0:T(8,128)(2,1)}), bf16[8,2,24,768]{3,2,1,0:T(8,128)(2,1)}, u32[]{:S(2)}, u32[]{:S(2)}) async-start(bf16[8,2,24,768]{3,2,1,0:T(8,128)(2,1)} %copy-done.13), calls=%async_computation | async-start | bytes 1179648 | tf_op jit(solution)/shard_map/all_to_all | solution.py:303
  9.4 0.8 slice_bitcast_fusion.7
  10.2 9.4 %all-to-all-done = bf16[8,2,24,768]{3,2,1,0:T(8,128)(2,1)} async-done(((bf16[8,2,24,768]{3,2,1,0:T(8,128)(2,1)}), bf16[8,2,24,768]{3,2,1,0:T(8,128)(2,1)}, u32[]{:S(2)}, u32[]{:S(2)}) %all-to-all-start) | async-done | bytes 589856 | tf_op jit(solution)/shard_map/all_to_all | solution.py:303
  19.6 1.2 convert_reduce_fusion.1.st_ref
  20.8 1.3 copy-done.22
  22.1 4.8 %norm_lon.2 = (bf16[96,24,768]{2,1,0:T(8,128)(2,1)S(1)}, bf16[16,48,2304]{2,1,0:T(8,128)(2,1)S(1)}) custom-call(f32[1]{0:T(128)} %constant.29.clone.1.scale_ref.refs_0_, f32[96]{0:T(128)S(1)} %get-tuple-element.35.gain_ref, f32[96]{0:T(128)S(1)} %get-tuple-element.30.shift_ref, bf16[96,24,768]{2,1,0:T(8,128)(2,1)S(1)} %copy-done.1, ...), custom_call_target="tpu_custom_call" | custom-call | flops 3000000000 | bytes 10000000 | tf_op jit(solution)/shard_map/norm_lon/pallas_call | solution.py:250
  27.0 1.8 copy-done.7
  28.7 1.8 copy-done.11
  30.5 7.9 %all-to-all-start.1 = ((bf16[16,48,2304]{2,1,0:T(8,128)(2,1)}), bf16[16,48,2304]{2,1,0:T(8,128)(2,1)}, u32[]{:S(2)}, u32[]{:S(2)}) async-start(bf16[16,48,2304]{2,1,0:T(8,128)(2,1)} %copy-done.11), calls=%async_computation.1 | async-start | bytes 7077888 | tf_op jit(solution)/shard_map/all_to_all | solution.py:287
  38.5 1.5 slice_bitcast_fusion.2
  40.0 43.0 %all-to-all-done.1.r_ref = bf16[16,48,2304]{2,1,0:T(8,128)(2,1)} async-done(((bf16[16,48,2304]{2,1,0:T(8,128)(2,1)}), bf16[16,48,2304]{2,1,0:T(8,128)(2,1)}, u32[]{:S(2)}, u32[]{:S(2)}) %all-to-all-start.1) | async-done | bytes 3538976 | tf_op jit(solution)/shard_map/all_to_all | solution.py:287
  83.1 0.8 copy-done.18
  83.9 0.8 copy-done.19
  84.7 1.3 copy-done.20
  85.9 1.1 copy-done.24
  87.0 18.3 %spectral.2 = bf16[16,48,2304]{2,1,0:T(8,128)(2,1)S(1)} custom-call(bf16[16,48,2304]{2,1,0:T(8,128)(2,1)} %all-to-all-done.1.r_ref, bf16[2,1,96,96]{3,2,1,0:T(8,128)(2,1)S(1)} %copy-done.19, bf16[2,1,96]{2,1,0:T(2,128)(2,1)S(1)} %copy.28.ba_ref, bf16[2,1,96,96]{3,2,1,0:T(8,128)(2,1)S(1)} %copy-done.18, bf16[384,768]{1,0:T(8,128)(2,1)S(1)} %copy-done.24, ...), custom_call_target="tpu_custom_call" | custom-call | flops 12000000000 | bytes 10000000 | tf_op jit(solution)/shard_map/spectral/pallas_call | solution.py:116
  105.3 49.8 %all_to_all.40.refs_1_ = bf16[16,48,2304]{2,1,0:T(8,128)(2,1)S(1)} all-to-all(bf16[16,48,2304]{2,1,0:T(8,128)(2,1)S(1)} %spectral.2), channel_id=1, replica_groups=mesh['lat_0'=4,'lat_1'=4,'ch_0'=4,'ch_1'=2] {'lat_0','lat_1'}, dimensions={0} | all-to-all | bytes 7077888 | tf_op jit(solution)/shard_map/all_to_all | solution.py:287
  155.1 7.5 %spatial.2 = (bf16[96,24,768]{2,1,0:T(8,128)(2,1)S(1)}, bf16[8,2,24,768]{3,2,1,0:T(8,128)(2,1)S(1)}) custom-call(f32[1]{0:T(128)} %constant.29.clone.1.scale_ref.refs_0_, bf16[16,48,2304]{2,1,0:T(8,128)(2,1)S(1)} %all_to_all.40.refs_1_, bf16[96,24,768]{2,1,0:T(8,128)(2,1)S(1)} %copy-done.1, bf16[96,24,768]{2,1,0:T(8,128)(2,1)S(1)} %copy-done.8, ...), custom_call_target="tpu_custom_call" | custom-call | flops 3000000000 | bytes 15000000 | tf_op jit(solution)/shard_map/spatial/pallas_call | solution.py:178
  162.6 1.8 copy-done.4
  164.4 0.8 copy-done.14
  165.2 10.1 %all-to-all-start.3 = ((bf16[8,2,24,768]{3,2,1,0:T(8,128)(2,1)}), bf16[8,2,24,768]{3,2,1,0:T(8,128)(2,1)S(1)}, u32[]{:S(2)}, u32[]{:S(2)}) async-start(bf16[8,2,24,768]{3,2,1,0:T(8,128)(2,1)} %copy-done.14), calls=%async_computation.3 | async-start | bytes 1179648 | tf_op jit(solution)/shard_map/all_to_all | solution.py:303
  175.3 10.0 %all-to-all-done.3 = bf16[8,2,24,768]{3,2,1,0:T(8,128)(2,1)S(1)} async-done(((bf16[8,2,24,768]{3,2,1,0:T(8,128)(2,1)}), bf16[8,2,24,768]{3,2,1,0:T(8,128)(2,1)S(1)}, u32[]{:S(2)}, u32[]{:S(2)}) %all-to-all-start.3) | async-done | bytes 589856 | tf_op jit(solution)/shard_map/all_to_all | solution.py:303
  185.4 1.6 fusion.3
  187.1 1.3 pad_maximum_fusion
  188.5 9.7 %all_to_all.41 = f32[16,2,128]{2,1,0:T(2,128)S(1)} all-to-all(f32[16,2,128]{2,1,0:T(2,128)S(1)} %broadcast_in_dim_broadcast_in_dim.8), channel_id=1, replica_groups=mesh['lat_0'=4,'lat_1'=4,'ch_0'=4,'ch_1'=2] {'lat_0','lat_1'}, dimensions={0} | all-to-all | bytes 32768 | tf_op jit(solution)/shard_map/all_to_all | solution.py:282
  198.2 0.6 fusion.4
  200.1 2.0 copy-done.5
  202.1 1.3 copy-done.23
  203.4 4.8 %norm_lon.3 = (bf16[96,24,768]{2,1,0:T(8,128)(2,1)S(1)}, bf16[16,48,2304]{2,1,0:T(8,128)(2,1)S(1)}) custom-call(f32[1]{0:T(128)} %bitcast.11.scale_ref.refs_0_, f32[96]{0:T(128)S(1)} %get-tuple-element.36.gain_ref, f32[96]{0:T(128)S(1)} %get-tuple-element.29.shift_ref, bf16[96,24,768]{2,1,0:T(8,128)(2,1)S(1)} %copy-done.5, ...), custom_call_target="tpu_custom_call" | custom-call | flops 3000000000 | bytes 10000000 | tf_op jit(solution)/shard_map/norm_lon/pallas_call | solution.py:250
  208.3 1.8 copy-done.9
  210.0 1.8 copy-done.12
  211.8 3.8 %all-to-all-start.5 = ((bf16[16,48,2304]{2,1,0:T(8,128)(2,1)}), bf16[16,48,2304]{2,1,0:T(8,128)(2,1)S(1)}, u32[]{:S(2)}, u32[]{:S(2)}) async-start(bf16[16,48,2304]{2,1,0:T(8,128)(2,1)} %copy-done.12), calls=%async_computation.5 | async-start | bytes 7077888 | tf_op jit(solution)/shard_map/all_to_all | solution.py:287
  215.6 41.4 %all-to-all-done.5.r_ref = bf16[16,48,2304]{2,1,0:T(8,128)(2,1)S(1)} async-done(((bf16[16,48,2304]{2,1,0:T(8,128)(2,1)}), bf16[16,48,2304]{2,1,0:T(8,128)(2,1)S(1)}, u32[]{:S(2)}, u32[]{:S(2)}) %all-to-all-start.5) | async-done | bytes 3538976 | tf_op jit(solution)/shard_map/all_to_all | solution.py:287
  257.0 0.8 copy-done.16
  257.8 0.8 copy-done.17
  258.6 1.3 copy-done.21
  259.8 1.1 copy-done.25
  260.9 16.3 %spectral.3 = bf16[16,48,2304]{2,1,0:T(8,128)(2,1)S(1)} custom-call(bf16[16,48,2304]{2,1,0:T(8,128)(2,1)S(1)} %all-to-all-done.5.r_ref, bf16[2,1,96,96]{3,2,1,0:T(8,128)(2,1)S(1)} %copy-done.17, bf16[2,1,96]{2,1,0:T(2,128)(2,1)S(1)} %copy.32.ba_ref, bf16[2,1,96,96]{3,2,1,0:T(8,128)(2,1)S(1)} %copy-done.16, bf16[384,768]{1,0:T(8,128)(2,1)S(1)} %copy-done.25, ...), custom_call_target="tpu_custom_call" | custom-call | flops 12000000000 | bytes 10000000 | tf_op jit(solution)/shard_map/spectral/pallas_call | solution.py:116
  277.2 45.7 %all_to_all.42.refs_1_ = bf16[16,48,2304]{2,1,0:T(8,128)(2,1)S(1)} all-to-all(bf16[16,48,2304]{2,1,0:T(8,128)(2,1)S(1)} %spectral.3), channel_id=1, replica_groups=mesh['lat_0'=4,'lat_1'=4,'ch_0'=4,'ch_1'=2] {'lat_0','lat_1'}, dimensions={0} | all-to-all | bytes 7077888 | tf_op jit(solution)/shard_map/all_to_all | solution.py:287
  322.9 7.5 %spatial.3 = (bf16[96,24,768]{2,1,0:T(8,128)(2,1)S(1)}, f32[24,768]{1,0:T(8,128)S(1)}) custom-call(f32[1]{0:T(128)} %bitcast.11.scale_ref.refs_0_, bf16[16,48,2304]{2,1,0:T(8,128)(2,1)S(1)} %all_to_all.42.refs_1_, bf16[96,24,768]{2,1,0:T(8,128)(2,1)S(1)} %copy-done.6, bf16[96,24,768]{2,1,0:T(8,128)(2,1)S(1)} %copy-done.10, bf16[768,768]{1,0:T(8,128)(2,1)S(1)} %copy-done.3), custom_call_target="tpu_custom_call" | custom-call | flops 3000000000 | bytes 15000000 | tf_op jit(solution)/shard_map/spatial/pallas_call | solution.py:178
  330.4 0.7 multiply_reduce_fusion
  331.1 0.7 broadcast_in_dim_broadcast_in_dim.9
  331.7 18.7 %all_to_all.43 = f32[128,1,128]{2,1,0:T(1,128)} all-to-all(f32[128,1,128]{2,1,0:T(1,128)S(1)} %broadcast_in_dim_broadcast_in_dim.9), channel_id=1, replica_groups=mesh['lat_0'=4,'lat_1'=4,'ch_0'=4,'ch_1'=2] {'lat_0','lat_1','ch_0','ch_1'}, dimensions={0} | all-to-all | bytes 131072 | tf_op jit(solution)/shard_map/all_to_all | solution.py:282
  350.4 0.9 reduce_sum.71
  352.1 3.0 final_scale.1
  (42 shorter events, 0.3 us)
Async XLA Ops:
  0.0 2.0 copy-start
  2.0 18.7 %copy-start.1 = (bf16[96,24,768]{2,1,0:T(8,128)(2,1)S(1)}, bf16[96,24,768]{2,1,0:T(8,128)(2,1)}, u32[]{:S(2)}) copy-start(bf16[96,24,768]{2,1,0:T(8,128)(2,1)} %refs_2_.1) | copy-start | bytes 10616836
  2.8 0.8 copy-start.13
  3.6 15.9 %all-to-all-start = ((bf16[8,2,24,768]{3,2,1,0:T(8,128)(2,1)}), bf16[8,2,24,768]{3,2,1,0:T(8,128)(2,1)}, u32[]{:S(2)}, u32[]{:S(2)}) async-start(bf16[8,2,24,768]{3,2,1,0:T(8,128)(2,1)} %copy-done.13), calls=%async_computation | async-start | bytes 1179648 | tf_op jit(solution)/shard_map/all_to_all | solution.py:303
  20.7 6.2 %copy-start.15 = (f32[2,24,768]{2,1,0:T(8,128)}, f32[2,24,768]{2,1,0:T(8,128)S(1)}, u32[]{:S(2)}) copy-start(f32[2,24,768]{2,1,0:T(8,128)S(1)} %convert_reduce_fusion.1.st_ref) | copy-start | bytes 442372
  20.8 1.3 copy-start.22
  26.9 1.8 copy-start.7
  28.7 1.8 copy-start.11
  30.5 8.0 %copy-start.26 = (bf16[2,2,1,96]{3,1,2,0:T(2,128)(2,1)S(1)}, bf16[2,2,1,96]{3,1,2,0:T(2,128)(2,1)}, u32[]{:S(2)}) copy-start(bf16[2,2,1,96]{3,1,2,0:T(2,128)(2,1)} %param.13) | copy-start | bytes 2308
  30.5 52.6 %all-to-all-start.1 = ((bf16[16,48,2304]{2,1,0:T(8,128)(2,1)}), bf16[16,48,2304]{2,1,0:T(8,128)(2,1)}, u32[]{:S(2)}, u32[]{:S(2)}) async-start(bf16[16,48,2304]{2,1,0:T(8,128)(2,1)} %copy-done.11), calls=%async_computation.1 | async-start | bytes 7077888 | tf_op jit(solution)/shard_map/all_to_all | solution.py:287
  83.1 0.8 copy-start.18
  83.9 0.8 copy-start.19
  84.7 1.3 copy-start.20
  85.9 1.1 copy-start.24
  105.3 49.8 %copy-start.2 = (bf16[768,768]{1,0:T(8,128)(2,1)S(1)}, bf16[768,768]{1,0:T(8,128)(2,1)}, u32[]{:S(2)}) copy-start(bf16[768,768]{1,0:T(8,128)(2,1)} %constant.32.clone.refs_4_) | copy-start | bytes 3538948
  105.3 49.8 %copy-start.8 = (bf16[96,24,768]{2,1,0:T(8,128)(2,1)S(1)}, bf16[96,24,768]{2,1,0:T(8,128)(2,1)}, u32[]{:S(2)}) copy-start(bf16[96,24,768]{2,1,0:T(8,128)(2,1)} %copy-done.7) | copy-start | bytes 10616836
  162.6 1.8 copy-start.4
  164.4 0.8 copy-start.14
  165.2 20.1 %all-to-all-start.3 = ((bf16[8,2,24,768]{3,2,1,0:T(8,128)(2,1)}), bf16[8,2,24,768]{3,2,1,0:T(8,128)(2,1)S(1)}, u32[]{:S(2)}, u32[]{:S(2)}) async-start(bf16[8,2,24,768]{3,2,1,0:T(8,128)(2,1)} %copy-done.14), calls=%async_computation.3 | async-start | bytes 1179648 | tf_op jit(solution)/shard_map/all_to_all | solution.py:303
  200.1 2.0 copy-start.5
  202.1 1.3 copy-start.23
  208.2 1.8 copy-start.9
  210.0 1.8 copy-start.12
  211.8 45.2 %all-to-all-start.5 = ((bf16[16,48,2304]{2,1,0:T(8,128)(2,1)}), bf16[16,48,2304]{2,1,0:T(8,128)(2,1)S(1)}, u32[]{:S(2)}, u32[]{:S(2)}) async-start(bf16[16,48,2304]{2,1,0:T(8,128)(2,1)} %copy-done.12), calls=%async_computation.5 | async-start | bytes 7077888 | tf_op jit(solution)/shard_map/all_to_all | solution.py:287
  257.0 0.8 copy-start.16
  257.8 0.8 copy-start.17
  258.6 1.3 copy-start.21
  259.8 1.1 copy-start.25
  260.9 62.0 %copy-start.10 = (bf16[96,24,768]{2,1,0:T(8,128)(2,1)S(1)}, bf16[96,24,768]{2,1,0:T(8,128)(2,1)}, u32[]{:S(2)}) copy-start(bf16[96,24,768]{2,1,0:T(8,128)(2,1)} %copy-done.9) | copy-start | bytes 10616836
  277.2 45.7 %copy-start.3 = (bf16[768,768]{1,0:T(8,128)(2,1)S(1)}, bf16[768,768]{1,0:T(8,128)(2,1)}, u32[]{:S(2)}) copy-start(bf16[768,768]{1,0:T(8,128)(2,1)} %constant.32.clone.refs_4_) | copy-start | bytes 3538948
  277.2 45.7 %copy-start.6 = (bf16[96,24,768]{2,1,0:T(8,128)(2,1)S(1)}, bf16[96,24,768]{2,1,0:T(8,128)(2,1)}, u32[]{:S(2)}) copy-start(bf16[96,24,768]{2,1,0:T(8,128)(2,1)} %copy-done.4) | copy-start | bytes 10616836

commit v3 on v1

v3 whole, which is shorter than its diff:
```python
import math

import jax
import jax.numpy as jnp
import numpy as np
from jax import lax
from jax.experimental import pallas as pl
from jax.experimental.pallas import tpu as pltpu
from jax.sharding import Mesh
from jax.sharding import PartitionSpec as P

CH = ("ch_0", "ch_1")
LAT = ("lat_0", "lat_1")
LAT_CH = LAT + CH
NORM_EPS = 1e-05
CH_ALL = 768
GROUPS = 6
MIX_STEP = 8
BIG = 60 << 20
F32, BF16 = jnp.float32, jnp.bfloat16
VM = pl.BlockSpec(memory_space=pltpu.VMEM)
SM = pl.BlockSpec(memory_space=pltpu.SMEM)
HBM = pl.BlockSpec(memory_space=pl.ANY)


def host_tables():
    def trig(length, freqs):
        n = np.arange(length)
        a = (n[:, None] * freqs[None, :] % length) * (2.0*math.pi/length)
        s = 1.0/math.sqrt(length)
        bf = jnp.bfloat16
        return (np.cos(a)*s).astype(bf), (np.sin(a)*s).astype(bf)
    c, s = trig(384, np.arange(384))
    tf = np.concatenate([c, s], 1)
    re = np.concatenate([c.T, -s.T], 1).reshape(16, 24, 768)
    im = np.concatenate([s.T, c.T], 1).reshape(16, 24, 768)
    ti = np.stack([re, im], 1).reshape(768, 768)
    lc, ls = trig(768, np.arange(384))
    t = np.concatenate([lc.T, -ls.T], 0)
    return tf, ti, t


def lanes_of(g):
    return pl.ds(pl.multiple_of(g * 384, 384), 384)


def chans_of(g):
    return pl.ds(pl.multiple_of(g * 16, 16), 16)


def exchange_into(xs, unit, put):
    for c in range(len(xs)):
        put(c, jnp.concatenate([x[:, unit * c : unit * (c + 1)] for x in xs], axis=1))


def dot(a, b, dims=((1,), (0,))):
    return lax.dot_general(a, b, (dims, ((), ())), preferred_element_type=F32)


def params(limit=BIG):
    return pltpu.CompilerParams(vmem_limit_bytes=limit)


def cost(flops, moved):
    return pl.CostEstimate(flops=flops, bytes_accessed=moved, transcendentals=0)


def put_stats(st_ref, sums, squares):
    for dest in range(st_ref.shape[0]):
        st_ref[dest, 0] = sums.astype(BF16)
        st_ref[dest, 1] = squares.astype(BF16)


def first_stats_kernel(v_ref, st_ref, sum_ref, sq_ref):
    g = pl.program_id(0)

    @pl.when(g == 0)
    def _():
        sum_ref[...] = jnp.zeros_like(sum_ref)
        sq_ref[...] = jnp.zeros_like(sq_ref)

    v = v_ref[...].astype(F32)
    sum_ref[...] += jnp.sum(v, axis=0)
    sq_ref[...] += jnp.sum(v * v, axis=0)

    @pl.when(g == pl.num_programs(0) - 1)
    def _():
        put_stats(st_ref, sum_ref[...], sq_ref[...])


def first_stats(v):
    plane = v.shape[1:]
    return pl.pallas_call(
        first_stats_kernel,
        out_shape=jax.ShapeDtypeStruct((8, 2, *plane), BF16),
        grid=(4,),
        in_specs=[pl.BlockSpec((24, *plane), lambda g: (g, 0, 0))],
        out_specs=pl.BlockSpec((8, 2, *plane), lambda g: (0, 0, 0, 0)),
        scratch_shapes=[pltpu.VMEM(plane, F32), pltpu.VMEM(plane, F32)],
        compiler_params=params(),
        cost_estimate=cost(6 * 10**6, 4 * 10**6),
        name="first_stats",
    )(v)


def gather_stats(st_ref):
    return tuple(sum(st_ref[d, i].astype(F32) for d in range(st_ref.shape[0])) for i in range(2))


def band_energy(area, squares):
    return jnp.sum(area * squares, keepdims=True)


def band_kernel(st_ref, area_ref, first_ref, sums_ref, pay_ref):
    total, squares = gather_stats(st_ref)
    sums_ref[0] = total
    sums_ref[1] = squares
    here = jnp.broadcast_to(band_energy(area_ref[...], squares), (1, 128))
    for dest in range(pay_ref.shape[0]):
        pay_ref[dest, 0:1] = first_ref[...]
        pay_ref[dest, 1:2] = here


def band_sums(stats, area, first):
    plane = stats.shape[2:]
    return pl.pallas_call(
        band_kernel,
        out_shape=(jax.ShapeDtypeStruct((2, *plane), F32), jax.ShapeDtypeStruct((16, 2, 128), F32)),
        in_specs=[VM] * 3,
        out_specs=(VM, VM),
        compiler_params=params(8 << 20),
        cost_estimate=cost(10**6, 10**6),
        name="band_sums",
    )(stats, area, first)


def layer_scale(pay_ref):
    both = jnp.sum(pay_ref[...], axis=0)
    return jnp.sqrt(both[0:1] / both[1:2])[0, 0]


def norm_body(layer, scale, total, squares, refs):
    gain_ref, shift_ref, v_hbm, tw_ref, n_hbm, o_hbm, v_ref, n_ref, o_ref, mean_ref, inv_ref, sems = refs
    loads = [pltpu.make_async_copy(v_hbm.at[chans_of(g)], v_ref.at[chans_of(g)], sems.at[g]) for g in range(GROUPS)]
    for load in loads:
        load.start()
    mean = total / CH_ALL
    spread = squares / CH_ALL - mean * mean
    mean_ref[...] = mean
    inv_ref[...] = scale * lax.rsqrt(spread * (scale * scale) + NORM_EPS)
    stores = []
    for g in range(GROUPS):
        loads[g].wait()
        mean, inv = mean_ref[...], inv_ref[...]
        rows = []
        for c in range(16 * g, 16 * g + 16):
            rows.append((v_ref[c].astype(F32) - mean) * inv * gain_ref[layer, c] + shift_ref[layer, c])
        x = jnp.concatenate(rows, axis=0).astype(BF16)
        n_ref[chans_of(g)] = x.astype(F32).reshape(16, 24, 768).astype(BF16)
        out = dot(tw_ref[...], x, ((1,), (1,)))
        o_ref[:, :, lanes_of(g)] = out.astype(BF16).reshape(16, 48, 384)
        for k, (src, dst, at) in enumerate(((n_ref, n_hbm, (chans_of(g),)), (o_ref, o_hbm, (slice(None), slice(None), lanes_of(g))))):
            store = pltpu.make_async_copy(src.at[at], dst.at[at], sems.at[GROUPS * (k + 1) + g])
            store.start()
            stores.append(store)
    for store in stores:
        store.wait()


def norm_first_kernel(gain_ref, shift_ref, v_hbm, tw_ref, st_ref, area_ref, n_hbm, o_hbm, band_ref, *rest):
    total, squares = gather_stats(st_ref)
    band_ref[...] = jnp.broadcast_to(band_energy(area_ref[...], squares), (1, 128))
    norm_body(0, 1.0, total, squares, (gain_ref, shift_ref, v_hbm, tw_ref, n_hbm, o_hbm, *rest))


def norm_later_kernel(layer, gain_ref, shift_ref, v_hbm, tw_ref, sums_ref, pay_ref, n_hbm, o_hbm, *rest):
    scale = layer_scale(pay_ref)
    norm_body(layer, scale, sums_ref[0], sums_ref[1], (gain_ref, shift_ref, v_hbm, tw_ref, n_hbm, o_hbm, *rest))


def norm_lon(layer, gain, shift, v, tw, stats, other):
    plane = v.shape[1:]
    pieces = (16, 48, 2304)
    outs = [jax.ShapeDtypeStruct(v.shape, BF16), jax.ShapeDtypeStruct(pieces, BF16)]
    specs = [HBM, HBM]
    if layer == 0:
        kernel = norm_first_kernel
        outs.append(jax.ShapeDtypeStruct((1, 128), F32))
        specs.append(VM)
    else:

        def kernel(*refs):
            norm_later_kernel(layer, *refs)

    return pl.pallas_call(
        kernel,
        out_shape=tuple(outs),
        in_specs=[SM, SM, HBM, VM, VM, VM],
        out_specs=tuple(specs),
        scratch_shapes=[
            pltpu.VMEM(v.shape, BF16),
            pltpu.VMEM(v.shape, BF16),
            pltpu.VMEM(pieces, BF16),
            pltpu.VMEM(plane, F32),
            pltpu.VMEM(plane, F32),
            pltpu.SemaphoreType.DMA((3 * GROUPS,)),
        ],
        compiler_params=params(),
        cost_estimate=cost(3 * 10**9, 10**7),
        name="norm_lon",
    )(gain, shift, v, tw, stats, other)


def complex_weight(w_ref):
    re, im = (w_ref[part].astype(F32).T for part in range(2))
    rows = [jnp.concatenate([re, -im], axis=1), jnp.concatenate([im, re], axis=1)]
    return jnp.concatenate(rows, axis=0).astype(BF16)


def spectral_kernel(
    layer, r_hbm, wa_hbm, ba_ref, wb_hbm, tf_hbm, ti_hbm, o_hbm,
    r_ref, o_ref, g_ref, f_ref, h_ref, wa_ref, wb_ref, tf_ref, ti_ref, sems, out_sems,
):
    def load(g):
        at = (slice(None), slice(None), lanes_of(g))
        return pltpu.make_async_copy(r_hbm.at[at], r_ref.at[at], sems.at[g])

    def store(g):
        at = (slice(None), slice(None), lanes_of(g))
        return pltpu.make_async_copy(o_ref.at[at], o_hbm.at[at], out_sems.at[g])

    load(0).start()
    tables = [
        pltpu.make_async_copy(src, dst, sems.at[GROUPS + i])
        for i, (src, dst) in enumerate(
            ((tf_hbm, tf_ref), (wa_hbm.at[layer, :, 0], wa_ref), (wb_hbm.at[layer, :, 0], wb_ref), (ti_hbm, ti_ref))
        )
    ]
    tables[0].start()
    for g in range(1, GROUPS):
        load(g).start()
    for table in tables[1:]:
        table.start()
    tables[0].wait()

    def forward(g, _):
        load(g).wait()
        l = lanes_of(g)
        for t in range(3):

            def put(c, v, t=t):
                g_ref[48 * c + 16 * t : 48 * c + 16 * t + 16, :] = v

            exchange_into([r_ref[p, 16 * t : 16 * t + 16, l] for p in range(16)], 24, put)
        prod = dot(g_ref[...], tf_ref[...]).reshape(16, 48, 768)
        re, im = prod[:, :24], prod[:, 24:]
        for k in range(3):
            a, b = slice(128 * k, 128 * k + 128), slice(384 + 128 * k, 512 + 128 * k)
            f_ref[k, l, :] = (re[:, :, a] + im[:, :, b]).reshape(384, 128)
            f_ref[3 + k, l, :] = (im[:, :, a] - re[:, :, b]).reshape(384, 128)
        return 0

    lax.fori_loop(0, GROUPS, forward, 0, unroll=3)
    for table in tables[1:]:
        table.wait()
    w1, w2 = complex_weight(wa_ref), complex_weight(wb_ref)
    b1 = jnp.concatenate([ba_ref[layer, part : part + 1].T for part in range(2)], axis=0)

    def mix(i, _):
        rows = [pl.ds(i * MIX_STEP + k, 96, stride=24) for k in range(MIX_STEP)]
        s = jnp.concatenate(
            [
                jnp.concatenate([f_ref[3 * part + k, row, :].astype(BF16) for row in rows for k in range(3)], axis=1)
                for part in range(2)
            ],
            axis=0,
        )
        hid = jnp.maximum(dot(w1, s) + b1, 0.0).astype(BF16)
        out = dot(w2, hid)
        out = jnp.where(out > 0.01, out - 0.01, jnp.where(out < -0.01, out + 0.01, 0.0))
        for n, row in enumerate(rows):
            for part in range(2):
                for k in range(3):
                    lane = 384 * n + 128 * k
                    h_ref[3 * part + k, row, :] = out[96 * part : 96 * part + 96, lane : lane + 128]
        return 0

    lax.fori_loop(0, 24 // MIX_STEP, mix, 0)

    def inverse(g, _):
        l = lanes_of(g)
        hb = jnp.concatenate([h_ref[k, l, :].astype(BF16) for k in range(6)], axis=1)
        out = dot(ti_ref[...], hb, ((1,), (1,)))
        o_ref[:, :, l] = out.astype(BF16).reshape(16, 48, 384)
        store(g).start()
        return 0

    lax.fori_loop(0, GROUPS, inverse, 0, unroll=2)
    for g in range(GROUPS):
        store(g).wait()


def spectral(layer, r, wa, ba, wb, tf, ti):
    def kernel(*refs):
        spectral_kernel(layer, *refs)

    weight = pltpu.VMEM((2, 96, 96), BF16)
    return pl.pallas_call(
        kernel,
        out_shape=jax.ShapeDtypeStruct(r.shape, BF16),
        in_specs=[HBM, HBM, VM, HBM, HBM, HBM],
        out_specs=HBM,
        scratch_shapes=[
            pltpu.VMEM(r.shape, BF16),
            pltpu.VMEM(r.shape, BF16),
            pltpu.VMEM((768, 384), BF16),
            pltpu.VMEM((6, 2304, 128), F32),
            pltpu.VMEM((6, 2304, 128), F32),
            weight,
            weight,
            pltpu.VMEM(tf.shape, BF16),
            pltpu.VMEM(ti.shape, BF16),
            pltpu.SemaphoreType.DMA((GROUPS + 4,)),
            pltpu.SemaphoreType.DMA((GROUPS,)),
        ],
        compiler_params=params(),
        cost_estimate=cost(12 * 10**9, 10**7),
        name="spectral",
    )(r, wa, ba, wb, tf, ti)


def spatial_kernel(first, last, *refs):
    refs = list(refs)
    pay_ref = None if first else refs.pop(0)
    area_ref = refs.pop(0) if last else None
    y_hbm, v_hbm, n_hbm, tl_hbm, u_hbm, st_ref = refs[:6]
    y_ref, v_ref, n_ref, tl_ref, u_ref, z_ref, sum_ref, sq_ref, sems, out_sems = refs[6:]

    def loads(g):
        at = (slice(None), slice(None), lanes_of(g))
        d = chans_of(g)
        return [
            pltpu.make_async_copy(src, dst, sems.at[k, g])
            for k, (src, dst) in enumerate(
                ((y_hbm.at[at], y_ref.at[at]), (v_hbm.at[d], v_ref.at[d]), (n_hbm.at[d], n_ref.at[d]))
            )
        ]

    def store(g):
        d = chans_of(g)
        return pltpu.make_async_copy(u_ref.at[d], u_hbm.at[d], out_sems.at[g])

    table = pltpu.make_async_copy(tl_hbm, tl_ref, sems.at[3, 0])
    for load in loads(0):
        load.start()
    table.start()
    for g in range(1, GROUPS):
        for load in loads(g):
            load.start()
    scale = 1.0 if first else layer_scale(pay_ref)
    mask = jnp.where(lax.broadcasted_iota(jnp.int32, (1, 384), 1) == 0, 1.0, 2.0)
    sum_ref[...] = jnp.zeros_like(sum_ref)
    sq_ref[...] = jnp.zeros_like(sq_ref)
    table.wait()

    def inverse(g, _):
        for load in loads(g):
            load.wait()
        l = lanes_of(g)
        for t in range(3):

            def put(c, v, t=t):
                z_ref[48 * c + 16 * t : 48 * c + 16 * t + 16, :] = v.astype(F32) * mask

            exchange_into([y_ref[p, 16 * t : 16 * t + 16, l] for p in range(16)], 24, put)
        z = z_ref[...].reshape(16, 48, 384)
        lhs = jnp.concatenate([z[:, :24], z[:, 24:]], axis=2).reshape(384, 768).astype(BF16)
        sp = dot(lhs, tl_ref[...]).reshape(16, 24, 768)
        d = chans_of(g)
        u = sp + n_ref[d].astype(F32) + v_ref[d].astype(F32) * scale
        u_ref[d] = u.astype(BF16)
        sum_ref[...] += jnp.sum(u, axis=0)
        sq_ref[...] += jnp.sum(u * u, axis=0)
        store(g).start()
        return 0

    lax.fori_loop(0, GROUPS, inverse, 0, unroll=2)
    if last:
        st_ref[...] = jnp.broadcast_to(band_energy(area_ref[...], sq_ref[...]).reshape(1, 1, 1), st_ref.shape)
    else:
        put_stats(st_ref, sum_ref[...], sq_ref[...])
    for g in range(GROUPS):
        store(g).wait()


def spatial(first, last, extra, y, v, n, tl):
    plane = v.shape[1:]
    stats = jax.ShapeDtypeStruct((128, 1, 128), F32) if last else jax.ShapeDtypeStruct((8, 2, *plane), BF16)

    def kernel(*refs):
        spatial_kernel(first, last, *refs)

    return pl.pallas_call(
        kernel,
        out_shape=(jax.ShapeDtypeStruct(v.shape, BF16), stats),
        in_specs=[VM] * len(extra) + [HBM] * 4,
        out_specs=(HBM, VM),
        scratch_shapes=[
            pltpu.VMEM(y.shape, BF16),
            pltpu.VMEM(v.shape, BF16),
            pltpu.VMEM(v.shape, BF16),
            pltpu.VMEM(tl.shape, BF16),
            pltpu.VMEM(v.shape, BF16),
            pltpu.VMEM((768, 384), F32),
            pltpu.VMEM(plane, F32),
            pltpu.VMEM(plane, F32),
            pltpu.SemaphoreType.DMA((4, GROUPS)),
            pltpu.SemaphoreType.DMA((GROUPS,)),
        ],
        compiler_params=params(),
        cost_estimate=cost(3 * 10**9, 15 * 10**6),
        name="spatial",
    )(*extra, y, v, n, tl)


def final_kernel(pay_ref, energy_ref, u_ref, o_ref):
    target = jnp.sum(pay_ref[...], axis=0)[0:1]
    energy = jnp.sum(energy_ref[...], axis=0)
    scale = jnp.sqrt(target / energy)[0, 0]
    d = pl.ds(pl.program_id(0) * o_ref.shape[0], o_ref.shape[0])
    o_ref[...] = (u_ref[d].astype(F32) * scale).astype(BF16)


def final_scale(pay, energy, u):
    return pl.pallas_call(
        final_kernel,
        out_shape=jax.ShapeDtypeStruct(u.shape, BF16),
        grid=(6,),
        in_specs=[VM] * 3,
        out_specs=pl.BlockSpec((16, *u.shape[1:]), lambda g: (g, 0, 0)),
        compiler_params=params(12 << 20),
        cost_estimate=cost(10**7, 7 * 10**6),
        name="final_scale",
    )(pay, energy, u)


def swap(x, axes):
    return lax.all_to_all(x, axes, split_axis=0, concat_axis=0, tiled=True)


def per_device(field_in, ln_gain, ln_shift, mix_first, mix_bias, mix_second):
    _, band_rows, lon_cells = field_in.shape
    lat_parts = lax.axis_size(LAT)
    lat_rows = band_rows * lat_parts
    tf, ti, tl = (jnp.asarray(t) for t in host_tables())
    tw = tl.reshape(2, lat_parts, 24, lon_cells).transpose(1, 0, 2, 3).reshape(768, lon_cells)
    row_pos = (lax.axis_index(LAT) * band_rows + jnp.arange(band_rows)).astype(F32)
    area = jnp.cos((row_pos + 0.5) * (math.pi / lat_rows) - 0.5 * math.pi)[:, None]
    bias = mix_bias.astype(F32).reshape(mix_bias.shape[0], 2, -1)
    layers = mix_first.shape[0]
    current, stats = field_in, first_stats(field_in)
    band = pay = None
    for layer in range(layers):
        stats = swap(stats, CH)
        if layer == 0:
            normed, lon, band = norm_lon(layer, ln_gain, ln_shift, current, tw, stats, area)
        else:
            sums, pay = band_sums(stats, area, band)
            pay = swap(pay, LAT)
            normed, lon = norm_lon(layer, ln_gain, ln_shift, current, tw, sums, pay)
        back = spectral(layer, swap(lon, LAT), mix_first, bias, mix_second, tf, ti)
        first, last = layer == 0, layer == layers - 1
        extra = ([] if first else [pay]) + ([area] if last else [])
        current, stats = spatial(first, last, extra, swap(back, LAT), current, normed, tl)
    return final_scale(pay, swap(stats, LAT_CH), current)


def solution(mesh):
    finer = Mesh(mesh.devices.reshape(4, 4, 4, 2), LAT_CH)
    in_specs = (
        P(CH, LAT, None),
        P(None, CH),
        P(None, CH),
        P(None, None, CH, None, None),
        P(None, None, CH, None),
        P(None, None, CH, None, None),
    )
    return jax.shard_map(
        per_device, mesh=finer, in_specs=in_specs, out_specs=P(CH, LAT, None), check_vma=False
    )
```

time: 379 us -> 357 us (0.942)
  blocking collectives: 124 us -> 188 us
  waiting for transfers between devices: 90 us -> 53.3 us
  other arithmetic: 23.5 us -> 1.25 us
  starting transfers between devices: 28.3 us -> 13.6 us
  local copies, waits for them, and re-layouts: 16.9 us -> 5.27 us
  Pallas kernels: 83.4 us -> 94.4 us
  matrix products: 8.85 us -> 0 us
    all_to_all x4 -> x6, blocking collectives: 124 us -> 188 us  [swap(): return lax.all_to_all(x, axes, split_axis=0, concat_axis=0, tiled=True)]
    all_to_all x4 -> x2, waiting for transfers between devices: 90 us -> 53.3 us  [swap(): return lax.all_to_all(x, axes, split_axis=0, concat_axis=0, tiled=True)]
    all_to_all x4 -> x2, starting transfers between devices: 28.3 us -> 13.6 us  [swap(): return lax.all_to_all(x, axes, split_axis=0, concat_axis=0, tiled=True)]
    pallas_call x4 -> x9, Pallas kernels: 83.4 us -> 94.4 us  [the longest x2 42.9 us: spectral(): pl.pallas_call(kernel, out_shape=jax.ShapeDtypeStruct(r.shape, BF16), in_...]
    convert_element_type x4 -> x0, other arithmetic: 9.9 us -> none  [the longest x2 4.75 us: per_device(): ((current.astype(jnp.float32) - mean) * inv_std * gain + shift).astype(jn...]
    dot_general x2 -> x0, matrix products: 8.85 us -> none  [dot(): lax.dot_general(a, b, (dims, ((), ())), preferred_element_type=jnp.float32)]
    reduce_sum x8 -> x0, other arithmetic: 7.39 us -> none  [the longest x2 4.64 us: per_device(): sums, squares = (jnp.sum(source, axis=0), jnp.sum(source * source, axis=0))]
    unnamed x34 -> x16, local copies, waits for them, and re-layouts: 8.6 us -> 5.27 us
  transfers between devices with their start and end apart: 4 -> 2, of which waited for: 4 -> 2; matrix products, arithmetic and copies ran while one was open for 4% -> 0% of each run, Pallas kernels for 0% -> 0%
where the time goes in v3:
time: 357 us; the launch traced here: 356 us
  blocking collectives  188 us (53%)
  Pallas kernels  94.4 us (26%)
  waiting for transfers between devices  53.3 us (15%)
  starting transfers between devices  13.6 us (4%)
  local copies, waits for them, and re-layouts  5.27 us (1%)
    all_to_all x6, blocking collectives, swap(): return lax.all_to_all(x, axes, split_axis=0, concat_axis=0, tiled=True)  188 us
    all_to_all x2, waiting for transfers between devices, swap(): return lax.all_to_all(x, axes, split_axis=0, concat_axis=0, tiled=True)  53.3 us
    pallas_call x2, Pallas kernels, spectral(): pl.pallas_call(kernel, out_shape=jax.ShapeDtypeStruct(r.shape, BF16), in_...  42.9 us
    pallas_call x2, Pallas kernels, spatial(): pl.pallas_call(kernel, out_shape=(jax.ShapeDtypeStruct(v.shape, BF16), st...  25.9 us
    pallas_call x2, Pallas kernels, norm_lon(): pl.pallas_call(kernel, out_shape=tuple(outs), in_specs=[SM, SM, HBM, VM,...  17.7 us
    all_to_all x2, starting transfers between devices, swap(): return lax.all_to_all(x, axes, split_axis=0, concat_axis=0, tiled=True)  13.6 us
  transfers between devices with their start and end apart: 2, of which 2 were waited for; matrix products, arithmetic and copies ran while one was open for 0% of the time, Pallas kernels for 0%

profile of v3, /device:TPU:1, one launch (start us, length us, event | category | flops | bytes accessed | tf_op | source)
XLA Modules:
  0.0 356.0 jit_solution(11483974410920475947)
XLA Ops:
  0.0 3.9 %first_stats.1 = bf16[8,2,24,768]{3,2,1,0:T(8,128)(2,1)} custom-call(bf16[96,24,768]{2,1,0:T(8,128)(2,1)} %refs_1_.5), custom_call_target="tpu_custom_call" | custom-call | flops 6000000 | bytes 4000000 | tf_op jit(solution)/shard_map/first_stats/pallas_call | solution.py:93
  3.9 5.8 %all-to-all-start = ((bf16[8,2,24,768]{3,2,1,0:T(8,128)(2,1)}), bf16[8,2,24,768]{3,2,1,0:T(8,128)(2,1)S(1)}, u32[]{:S(2)}, u32[]{:S(2)}) async-start(bf16[8,2,24,768]{3,2,1,0:T(8,128)(2,1)} %first_stats.1), calls=%async_computation | async-start | bytes 1179648 | tf_op jit(solution)/shard_map/all_to_all | solution.py:448
  9.7 0.7 add_cosine_fusion.area_ref.refs_1_
  10.3 9.4 %all-to-all-done.st_ref = bf16[8,2,24,768]{3,2,1,0:T(8,128)(2,1)S(1)} async-done(((bf16[8,2,24,768]{3,2,1,0:T(8,128)(2,1)}), bf16[8,2,24,768]{3,2,1,0:T(8,128)(2,1)S(1)}, u32[]{:S(2)}, u32[]{:S(2)}) %all-to-all-start) | async-done | bytes 589856 | tf_op jit(solution)/shard_map/all_to_all | solution.py:448
  19.7 0.0 copy-start.6
  19.7 0.8 copy-done.6
  20.5 9.2 %norm_lon.2 = (bf16[96,24,768]{2,1,0:T(8,128)(2,1)}, bf16[16,48,2304]{2,1,0:T(8,128)(2,1)}, f32[1,128]{1,0:T(1,128)}) custom-call(f32[2,96]{1,0:T(2,128)} %refs_0_.1, f32[2,96]{1,0:T(2,128)} %refs_1_.6, bf16[96,24,768]{2,1,0:T(8,128)(2,1)} %refs_1_.5, bf16[768,768]{1,0:T(8,128)(2,1)} %constant.35.tw_ref.refs_3_, bf16[8,2,24,768]{3,2,1,0:T(8,128)(2,1)} %copy-done.6, ...), custom_call_target="tpu_custom_call" | custom-call | flops 3000000000 | bytes 10000000 | tf_op jit(solution)/shard_map/norm_lon/pallas_call | solution.py:195
  29.7 0.0 copy-start.7
  29.7 7.8 %all-to-all-start.1 = ((bf16[16,48,2304]{2,1,0:T(8,128)(2,1)}), bf16[16,48,2304]{2,1,0:T(8,128)(2,1)S(1)}, u32[]{:S(2)}, u32[]{:S(2)}) async-start(bf16[16,48,2304]{2,1,0:T(8,128)(2,1)} %get-tuple-element.16), calls=%async_computation.1 | async-start | bytes 7077888 | tf_op jit(solution)/shard_map/all_to_all | solution.py:448
  37.5 0.0 copy-done.7
  37.5 0.6 bitcast_convert_fusion.refs_2_
  38.1 43.9 %all-to-all-done.1.refs_0_ = bf16[16,48,2304]{2,1,0:T(8,128)(2,1)S(1)} async-done(((bf16[16,48,2304]{2,1,0:T(8,128)(2,1)}), bf16[16,48,2304]{2,1,0:T(8,128)(2,1)S(1)}, u32[]{:S(2)}, u32[]{:S(2)}) %all-to-all-start.1) | async-done | bytes 3538976 | tf_op jit(solution)/shard_map/all_to_all | solution.py:448
  82.1 0.0 copy-start.5
  82.1 1.8 copy-done.5
  83.8 21.4 %spectral.2 = bf16[16,48,2304]{2,1,0:T(8,128)(2,1)} custom-call(bf16[16,48,2304]{2,1,0:T(8,128)(2,1)} %copy-done.5, bf16[2,2,1,96,96]{4,3,2,1,0:T(8,128)(2,1)} %refs_1_.7, f32[2,2,96]{2,1,0:T(2,128)} %bitcast_convert_fusion.refs_2_, bf16[2,2,1,96,96]{4,3,2,1,0:T(8,128)(2,1)} %refs_3_.4, bf16[384,768]{1,0:T(8,128)(2,1)} %constant.26.clone.refs_4_, ...), custom_call_target="tpu_custom_call" | custom-call | flops 12000000000 | bytes 10000000 | tf_op jit(solution)/shard_map/spectral/pallas_call | solution.py:308
  105.3 49.8 %all_to_all.40.refs_0_ = bf16[16,48,2304]{2,1,0:T(8,128)(2,1)} all-to-all(bf16[16,48,2304]{2,1,0:T(8,128)(2,1)} %spectral.2), channel_id=1, replica_groups=mesh['lat_0'=4,'lat_1'=4,'ch_0'=4,'ch_1'=2] {'lat_0','lat_1'}, dimensions={0} | all-to-all | bytes 7077888 | tf_op jit(solution)/shard_map/all_to_all | solution.py:448
  155.1 0.0 copy-start.2
  155.1 0.0 copy-start.3
  155.1 12.7 %spatial.2 = (bf16[96,24,768]{2,1,0:T(8,128)(2,1)}, bf16[8,2,24,768]{3,2,1,0:T(8,128)(2,1)}) custom-call(bf16[16,48,2304]{2,1,0:T(8,128)(2,1)} %all_to_all.40.refs_0_, bf16[96,24,768]{2,1,0:T(8,128)(2,1)} %refs_1_.5, bf16[96,24,768]{2,1,0:T(8,128)(2,1)} %get-tuple-element.17.refs_2_, bf16[768,768]{1,0:T(8,128)(2,1)} %constant.28.clone.refs_3_.refs_5_), custom_call_target="tpu_custom_call" | custom-call | flops 3000000000 | bytes 15000000 | tf_op jit(solution)/shard_map/spatial/pallas_call | solution.py:403
  167.8 20.4 %all_to_all.41.st_ref = bf16[8,2,24,768]{3,2,1,0:T(8,128)(2,1)S(1)} all-to-all(bf16[8,2,24,768]{3,2,1,0:T(8,128)(2,1)} %get-tuple-element.18), channel_id=1, replica_groups=mesh['lat_0'=4,'lat_1'=4,'ch_0'=4,'ch_1'=2] {'ch_0','ch_1'}, dimensions={0} | all-to-all | bytes 1179648 | tf_op jit(solution)/shard_map/all_to_all | solution.py:448
  188.2 0.0 copy-done.2
  188.2 0.0 copy-done.3
  188.2 0.2 band_sums.1
  188.4 0.0 copy-start.4
  188.4 0.6 copy-done.4
  189.1 9.7 %all_to_all.42.refs_5_.refs_0_.pay_ref = f32[16,2,128]{2,1,0:T(2,128)} all-to-all(f32[16,2,128]{2,1,0:T(2,128)S(1)} %get-tuple-element.20), channel_id=1, replica_groups=mesh['lat_0'=4,'lat_1'=4,'ch_0'=4,'ch_1'=2] {'lat_0','lat_1'}, dimensions={0} | all-to-all | bytes 32768 | tf_op jit(solution)/shard_map/all_to_all | solution.py:448
  198.7 8.5 %norm_lon.3 = (bf16[96,24,768]{2,1,0:T(8,128)(2,1)}, bf16[16,48,2304]{2,1,0:T(8,128)(2,1)}) custom-call(f32[2,96]{1,0:T(2,128)} %refs_0_.1, f32[2,96]{1,0:T(2,128)} %refs_1_.6, bf16[96,24,768]{2,1,0:T(8,128)(2,1)} %get-tuple-element.21.refs_2_.refs_3_, bf16[768,768]{1,0:T(8,128)(2,1)} %constant.35.tw_ref.refs_3_, f32[2,24,768]{2,1,0:T(8,128)} %copy-done.4, ...), custom_call_target="tpu_custom_call" | custom-call | flops 3000000000 | bytes 10000000 | tf_op jit(solution)/shard_map/norm_lon/pallas_call | solution.py:195
  207.3 45.5 %all_to_all.43.refs_0_ = bf16[16,48,2304]{2,1,0:T(8,128)(2,1)} all-to-all(bf16[16,48,2304]{2,1,0:T(8,128)(2,1)} %get-tuple-element.23), channel_id=1, replica_groups=mesh['lat_0'=4,'lat_1'=4,'ch_0'=4,'ch_1'=2] {'lat_0','lat_1'}, dimensions={0} | all-to-all | bytes 7077888 | tf_op jit(solution)/shard_map/all_to_all | solution.py:448
  252.7 21.4 %spectral.3 = bf16[16,48,2304]{2,1,0:T(8,128)(2,1)} custom-call(bf16[16,48,2304]{2,1,0:T(8,128)(2,1)} %all_to_all.43.refs_0_, bf16[2,2,1,96,96]{4,3,2,1,0:T(8,128)(2,1)} %refs_1_.7, f32[2,2,96]{2,1,0:T(2,128)} %bitcast_convert_fusion.refs_2_, bf16[2,2,1,96,96]{4,3,2,1,0:T(8,128)(2,1)} %refs_3_.4, bf16[384,768]{1,0:T(8,128)(2,1)} %constant.26.clone.refs_4_, ...), custom_call_target="tpu_custom_call" | custom-call | flops 12000000000 | bytes 10000000 | tf_op jit(solution)/shard_map/spectral/pallas_call | solution.py:308
  274.2 44.2 %all_to_all.44.refs_2_ = bf16[16,48,2304]{2,1,0:T(8,128)(2,1)} all-to-all(bf16[16,48,2304]{2,1,0:T(8,128)(2,1)} %spectral.3), channel_id=1, replica_groups=mesh['lat_0'=4,'lat_1'=4,'ch_0'=4,'ch_1'=2] {'lat_0','lat_1'}, dimensions={0} | all-to-all | bytes 7077888 | tf_op jit(solution)/shard_map/all_to_all | solution.py:448
  318.3 0.0 copy-start.1
  318.3 13.2 %spatial.3 = (bf16[96,24,768]{2,1,0:T(8,128)(2,1)}, f32[128,1,128]{2,1,0:T(1,128)}) custom-call(f32[16,2,128]{2,1,0:T(2,128)} %all_to_all.42.refs_5_.refs_0_.pay_ref, f32[24,1]{1,0:T(8,128)} %add_cosine_fusion.area_ref.refs_1_, bf16[16,48,2304]{2,1,0:T(8,128)(2,1)} %all_to_all.44.refs_2_, bf16[96,24,768]{2,1,0:T(8,128)(2,1)} %get-tuple-element.21.refs_2_.refs_3_, ...), custom_call_target="tpu_custom_call" | custom-call | flops 3000000000 | bytes 15000000 | tf_op jit(solution)/shard_map/spatial/pallas_call | solution.py:403
  331.6 18.6 %all_to_all.45.energy_ref = f32[128,1,128]{2,1,0:T(1,128)S(1)} all-to-all(f32[128,1,128]{2,1,0:T(1,128)} %get-tuple-element.25), channel_id=1, replica_groups=mesh['lat_0'=4,'lat_1'=4,'ch_0'=4,'ch_1'=2] {'lat_0','lat_1','ch_0','ch_1'}, dimensions={0} | all-to-all | bytes 131072 | tf_op jit(solution)/shard_map/all_to_all | solution.py:448
  350.2 0.0 copy-done.1
  350.2 0.0 copy-start
  350.2 2.0 copy-done
  352.2 3.8 %final_scale.1 = bf16[96,24,768]{2,1,0:T(8,128)(2,1)} custom-call(f32[16,2,128]{2,1,0:T(2,128)S(1)} %copy-done.1, f32[128,1,128]{2,1,0:T(1,128)S(1)} %all_to_all.45.energy_ref, bf16[96,24,768]{2,1,0:T(8,128)(2,1)S(1)} %copy-done), custom_call_target="tpu_custom_call" | custom-call | flops 10000000 | bytes 7000000 | tf_op jit(solution)/shard_map/final_scale/pallas_call | solution.py:435
Async XLA Ops:
  3.9 15.8 %all-to-all-start = ((bf16[8,2,24,768]{3,2,1,0:T(8,128)(2,1)}), bf16[8,2,24,768]{3,2,1,0:T(8,128)(2,1)S(1)}, u32[]{:S(2)}, u32[]{:S(2)}) async-start(bf16[8,2,24,768]{3,2,1,0:T(8,128)(2,1)} %first_stats.1), calls=%async_computation | async-start | bytes 1179648 | tf_op jit(solution)/shard_map/all_to_all | solution.py:448
  19.7 0.8 copy-start.6
  29.7 7.8 %copy-start.7 = (bf16[2,2,1,96]{3,1,2,0:T(2,128)(2,1)S(1)}, bf16[2,2,1,96]{3,1,2,0:T(2,128)(2,1)}, u32[]{:S(2)}) copy-start(bf16[2,2,1,96]{3,1,2,0:T(2,128)(2,1)} %param.13) | copy-start | bytes 2308
  29.7 52.3 %all-to-all-start.1 = ((bf16[16,48,2304]{2,1,0:T(8,128)(2,1)}), bf16[16,48,2304]{2,1,0:T(8,128)(2,1)S(1)}, u32[]{:S(2)}, u32[]{:S(2)}) async-start(bf16[16,48,2304]{2,1,0:T(8,128)(2,1)} %get-tuple-element.16), calls=%async_computation.1 | async-start | bytes 7077888 | tf_op jit(solution)/shard_map/all_to_all | solution.py:448
  82.1 1.8 copy-start.5
  155.1 33.1 %copy-start.2 = (f32[24,1]{1,0:T(8,128)S(1)}, f32[24,1]{1,0:T(8,128)}, u32[]{:S(2)}) copy-start(f32[24,1]{1,0:T(8,128)} %add_cosine_fusion.area_ref.refs_1_) | copy-start | bytes 292
  155.1 33.1 %copy-start.3 = (f32[1,128]{1,0:T(1,128)S(1)}, f32[1,128]{1,0:T(1,128)}, u32[]{:S(2)}) copy-start(f32[1,128]{1,0:T(1,128)} %get-tuple-element.19.first_ref) | copy-start | bytes 1540
  188.4 0.7 copy-start.4
  318.3 31.8 %copy-start.1 = (f32[16,2,128]{2,1,0:T(2,128)S(1)}, f32[16,2,128]{2,1,0:T(2,128)}, u32[]{:S(2)}) copy-start(f32[16,2,128]{2,1,0:T(2,128)} %all_to_all.42.refs_5_.refs_0_.pay_ref) | copy-start | bytes 49156
  350.2 2.0 copy-start

commit v4 on v3

v4 whole, which is shorter than its diff:
```python
import math

import jax
import jax.numpy as jnp
import numpy as np
from jax import lax
from jax.experimental import pallas as pl
from jax.experimental.pallas import tpu as pltpu
from jax.sharding import Mesh
from jax.sharding import PartitionSpec as P

CH = ("ch_0", "ch_1")
LAT = ("lat_0", "lat_1")
LAT_CH = LAT + CH
NORM_EPS = 1e-05
CH_ALL = 768
GROUPS = 6
MIX_STEP = 8
NORM_MIB, SPECTRAL_MIB, SPATIAL_MIB = 12, 24, 12
F32, BF16 = jnp.float32, jnp.bfloat16
VM = pl.BlockSpec(memory_space=pltpu.VMEM)
SM = pl.BlockSpec(memory_space=pltpu.SMEM)


def host_tables():
    def trig(length, freqs):
        n = np.arange(length)
        a = (n[:, None] * freqs[None, :] % length) * (2.0*math.pi/length)
        s = 1.0/math.sqrt(length)
        bf = jnp.bfloat16
        return (np.cos(a)*s).astype(bf), (np.sin(a)*s).astype(bf)
    c, s = trig(384, np.arange(384))
    tf = np.concatenate([c, s], 1)
    re = np.concatenate([c.T, -s.T], 1).reshape(16, 24, 768)
    im = np.concatenate([s.T, c.T], 1).reshape(16, 24, 768)
    ti = np.stack([re, im], 1).reshape(768, 768)
    lc, ls = trig(768, np.arange(384))
    t = np.concatenate([lc.T, -ls.T], 0)
    return tf, ti, t


def lanes_of(g):
    return pl.ds(pl.multiple_of(g * 384, 384), 384)


def chans_of(g):
    return pl.ds(pl.multiple_of(g * 16, 16), 16)


def exchange_into(xs, unit, put):
    for c in range(len(xs)):
        put(c, jnp.concatenate([x[:, unit * c : unit * (c + 1)] for x in xs], axis=1))


def dot(a, b, dims=((1,), (0,))):
    return lax.dot_general(a, b, (dims, ((), ())), preferred_element_type=F32)


def params(mib):
    return pltpu.CompilerParams(vmem_limit_bytes=mib << 20)


def cost(flops, moved):
    return pl.CostEstimate(flops=flops, bytes_accessed=moved, transcendentals=0)


def put_stats(st_ref, sums, squares):
    for dest in range(st_ref.shape[0]):
        st_ref[dest, 0] = sums.astype(BF16)
        st_ref[dest, 1] = squares.astype(BF16)


def first_stats_kernel(v_ref, st_ref, sum_ref, sq_ref):
    sum_ref[...] = jnp.zeros_like(sum_ref)
    sq_ref[...] = jnp.zeros_like(sq_ref)

    def group(g, _):
        v = v_ref[chans_of(g)].astype(F32)
        sum_ref[...] += jnp.sum(v, axis=0)
        sq_ref[...] += jnp.sum(v * v, axis=0)
        return 0

    lax.fori_loop(0, GROUPS, group, 0)
    put_stats(st_ref, sum_ref[...], sq_ref[...])


def first_stats(v):
    plane = v.shape[1:]
    return pl.pallas_call(
        first_stats_kernel,
        out_shape=jax.ShapeDtypeStruct((8, 2, *plane), BF16),
        in_specs=[VM],
        out_specs=VM,
        scratch_shapes=[pltpu.VMEM(plane, F32), pltpu.VMEM(plane, F32)],
        compiler_params=params(8),
        cost_estimate=cost(6 * 10**6, 4 * 10**6),
        name="first_stats",
    )(v)


def gather_stats(st_ref):
    return tuple(sum(st_ref[d, i].astype(F32) for d in range(st_ref.shape[0])) for i in range(2))


def band_energy(squares):
    rows = squares.shape[0]
    first_row = lax.axis_index(LAT) * rows
    row_pos = (first_row + lax.broadcasted_iota(jnp.int32, squares.shape, 0)).astype(F32)
    area = jnp.cos((row_pos + 0.5) * (math.pi / (rows * lax.axis_size(LAT))) - 0.5 * math.pi)
    return jnp.sum(area * squares, keepdims=True)


def band_kernel(st_ref, first_ref, sums_ref, pay_ref):
    total, squares = gather_stats(st_ref)
    sums_ref[0] = total
    sums_ref[1] = squares
    here = jnp.broadcast_to(band_energy(squares), (1, 128))
    for dest in range(pay_ref.shape[0]):
        pay_ref[dest, 0:1] = first_ref[...]
        pay_ref[dest, 1:2] = here


def band_sums(stats, first):
    plane = stats.shape[2:]
    return pl.pallas_call(
        band_kernel,
        out_shape=(jax.ShapeDtypeStruct((2, *plane), F32), jax.ShapeDtypeStruct((16, 2, 128), F32)),
        in_specs=[VM] * 2,
        out_specs=(VM, VM),
        compiler_params=params(8),
        cost_estimate=cost(10**6, 10**6),
        name="band_sums",
    )(stats, first)


def layer_scale(pay_ref):
    both = jnp.sum(pay_ref[...], axis=0)
    return jnp.sqrt(both[0:1] / both[1:2])[0, 0]


def norm_kernel(layer, gain_ref, shift_ref, v_ref, tw_ref, *refs):
    if layer == 0:
        st_ref, n_ref, o_ref, band_ref, mean_ref, inv_ref = refs
        scale = 1.0
        total, squares = gather_stats(st_ref)
        band_ref[...] = jnp.broadcast_to(band_energy(squares), (1, 128))
    else:
        sums_ref, pay_ref, n_ref, o_ref, mean_ref, inv_ref = refs
        scale = layer_scale(pay_ref)
        total, squares = sums_ref[0], sums_ref[1]
    mean = total / CH_ALL
    spread = squares / CH_ALL - mean * mean
    mean_ref[...] = mean
    inv_ref[...] = scale * lax.rsqrt(spread * (scale * scale) + NORM_EPS)

    def group(g, _):
        mean, inv = mean_ref[...], inv_ref[...]
        rows = []
        for i in range(16):
            c = g * 16 + i
            rows.append((v_ref[c].astype(F32) - mean) * inv * gain_ref[layer, c] + shift_ref[layer, c])
        x = jnp.concatenate(rows, axis=0).astype(BF16)
        n_ref[chans_of(g)] = x.astype(F32).reshape(16, 24, 768).astype(BF16)
        out = dot(tw_ref[...], x, ((1,), (1,)))
        o_ref[:, :, lanes_of(g)] = out.astype(BF16).reshape(16, 48, 384)
        return 0

    lax.fori_loop(0, GROUPS, group, 0, unroll=2)


def norm_lon(layer, gain, shift, v, tw, *stats):
    plane = v.shape[1:]
    outs = [jax.ShapeDtypeStruct(v.shape, BF16), jax.ShapeDtypeStruct((16, 48, 2304), BF16)]
    if layer == 0:
        outs.append(jax.ShapeDtypeStruct((1, 128), F32))

    def kernel(*refs):
        norm_kernel(layer, *refs)

    return pl.pallas_call(
        kernel,
        out_shape=tuple(outs),
        in_specs=[SM, SM] + [VM] * (2 + len(stats)),
        out_specs=(VM,) * len(outs),
        scratch_shapes=[pltpu.VMEM(plane, F32), pltpu.VMEM(plane, F32)],
        compiler_params=params(NORM_MIB),
        cost_estimate=cost(3 * 10**9, 10**7),
        name="norm_lon",
    )(gain, shift, v, tw, *stats)


def complex_weight(w_ref, layer):
    re, im = (w_ref[layer, part, 0].astype(F32).T for part in range(2))
    rows = [jnp.concatenate([re, -im], axis=1), jnp.concatenate([im, re], axis=1)]
    return jnp.concatenate(rows, axis=0).astype(BF16)


def spectral_kernel(layer, r_ref, wa_ref, ba_ref, wb_ref, tf_ref, ti_ref, o_ref, g_ref, f_ref, h_ref):
    def forward(g, _):
        l = lanes_of(g)
        for t in range(3):

            def put(c, v, t=t):
                g_ref[48 * c + 16 * t : 48 * c + 16 * t + 16, :] = v

            exchange_into([r_ref[p, 16 * t : 16 * t + 16, l] for p in range(16)], 24, put)
        prod = dot(g_ref[...], tf_ref[...]).reshape(16, 48, 768)
        re, im = prod[:, :24], prod[:, 24:]
        for k in range(3):
            a, b = slice(128 * k, 128 * k + 128), slice(384 + 128 * k, 512 + 128 * k)
            f_ref[k, l, :] = (re[:, :, a] + im[:, :, b]).reshape(384, 128)
            f_ref[3 + k, l, :] = (im[:, :, a] - re[:, :, b]).reshape(384, 128)
        return 0

    lax.fori_loop(0, GROUPS, forward, 0, unroll=3)
    w1, w2 = complex_weight(wa_ref, layer), complex_weight(wb_ref, layer)
    b1 = jnp.concatenate([ba_ref[layer, part].T for part in range(2)], axis=0)

    def mix(i, _):
        rows = [pl.ds(i * MIX_STEP + k, 96, stride=24) for k in range(MIX_STEP)]
        s = jnp.concatenate(
            [
                jnp.concatenate([f_ref[3 * part + k, row, :].astype(BF16) for row in rows for k in range(3)], axis=1)
                for part in range(2)
            ],
            axis=0,
        )
        hid = jnp.maximum(dot(w1, s) + b1, 0.0).astype(BF16)
        out = dot(w2, hid)
        out = jnp.where(out > 0.01, out - 0.01, jnp.where(out < -0.01, out + 0.01, 0.0))
        for n, row in enumerate(rows):
            for part in range(2):
                for k in range(3):
                    lane = 384 * n + 128 * k
                    h_ref[3 * part + k, row, :] = out[96 * part : 96 * part + 96, lane : lane + 128]
        return 0

    lax.fori_loop(0, 24 // MIX_STEP, mix, 0)

    def inverse(g, _):
        l = lanes_of(g)
        hb = jnp.concatenate([h_ref[k, l, :].astype(BF16) for k in range(6)], axis=1)
        out = dot(ti_ref[...], hb, ((1,), (1,)))
        o_ref[:, :, l] = out.astype(BF16).reshape(16, 48, 384)
        return 0

    lax.fori_loop(0, GROUPS, inverse, 0, unroll=3)


def spectral(layer, r, wa, ba, wb, tf, ti):
    def kernel(*refs):
        spectral_kernel(layer, *refs)

    return pl.pallas_call(
        kernel,
        out_shape=jax.ShapeDtypeStruct(r.shape, BF16),
        in_specs=[VM] * 6,
        out_specs=VM,
        scratch_shapes=[
            pltpu.VMEM((768, 384), BF16),
            pltpu.VMEM((6, 2304, 128), F32),
            pltpu.VMEM((6, 2304, 128), F32),
        ],
        compiler_params=params(SPECTRAL_MIB),
        cost_estimate=cost(12 * 10**9, 10**7),
        name="spectral",
    )(r, wa, ba, wb, tf, ti)


def spatial_kernel(first, last, *refs):
    refs = list(refs)
    scale = 1.0 if first else layer_scale(refs.pop(0))
    y_ref, v_ref, n_ref, tl_ref, u_ref, st_ref, z_ref, sum_ref, sq_ref = refs
    mask = jnp.where(lax.broadcasted_iota(jnp.int32, (1, 384), 1) == 0, 1.0, 2.0)
    sum_ref[...] = jnp.zeros_like(sum_ref)
    sq_ref[...] = jnp.zeros_like(sq_ref)

    def inverse(g, _):
        l = lanes_of(g)
        for t in range(3):

            def put(c, v, t=t):
                z_ref[48 * c + 16 * t : 48 * c + 16 * t + 16, :] = v.astype(F32) * mask

            exchange_into([y_ref[p, 16 * t : 16 * t + 16, l] for p in range(16)], 24, put)
        z = z_ref[...].reshape(16, 48, 384)
        lhs = jnp.concatenate([z[:, :24], z[:, 24:]], axis=2).reshape(384, 768).astype(BF16)
        sp = dot(lhs, tl_ref[...]).reshape(16, 24, 768)
        d = chans_of(g)
        u = sp + n_ref[d].astype(F32) + v_ref[d].astype(F32) * scale
        u_ref[d] = u.astype(BF16)
        sum_ref[...] += jnp.sum(u, axis=0)
        sq_ref[...] += jnp.sum(u * u, axis=0)
        return 0

    lax.fori_loop(0, GROUPS, inverse, 0, unroll=2)
    if last:
        st_ref[...] = jnp.broadcast_to(band_energy(sq_ref[...]).reshape(1, 1, 1), st_ref.shape)
    else:
        put_stats(st_ref, sum_ref[...], sq_ref[...])


def spatial(first, last, extra, y, v, n, tl):
    plane = v.shape[1:]
    stats = jax.ShapeDtypeStruct((128, 1, 128), F32) if last else jax.ShapeDtypeStruct((8, 2, *plane), BF16)

    def kernel(*refs):
        spatial_kernel(first, last, *refs)

    return pl.pallas_call(
        kernel,
        out_shape=(jax.ShapeDtypeStruct(v.shape, BF16), stats),
        in_specs=[VM] * (len(extra) + 4),
        out_specs=(VM, VM),
        scratch_shapes=[pltpu.VMEM((768, 384), F32), pltpu.VMEM(plane, F32), pltpu.VMEM(plane, F32)],
        compiler_params=params(SPATIAL_MIB),
        cost_estimate=cost(3 * 10**9, 15 * 10**6),
        name="spatial",
    )(*extra, y, v, n, tl)


def final_kernel(pay_ref, energy_ref, u_ref, o_ref):
    target = jnp.sum(pay_ref[...], axis=0)[0:1]
    energy = jnp.sum(energy_ref[...], axis=0)
    scale = jnp.sqrt(target / energy)[0, 0]
    d = pl.ds(pl.program_id(0) * o_ref.shape[0], o_ref.shape[0])
    o_ref[...] = (u_ref[d].astype(F32) * scale).astype(BF16)


def final_scale(pay, energy, u):
    return pl.pallas_call(
        final_kernel,
        out_shape=jax.ShapeDtypeStruct(u.shape, BF16),
        grid=(6,),
        in_specs=[VM] * 3,
        out_specs=pl.BlockSpec((16, *u.shape[1:]), lambda g: (g, 0, 0)),
        compiler_params=params(8),
        cost_estimate=cost(10**7, 7 * 10**6),
        name="final_scale",
    )(pay, energy, u)


def swap(x, axes):
    return lax.all_to_all(x, axes, split_axis=0, concat_axis=0, tiled=True)


def per_device(field_in, ln_gain, ln_shift, mix_first, mix_bias, mix_second):
    lon_cells = field_in.shape[-1]
    lat_parts = lax.axis_size(LAT)
    tf, ti, tl = (jnp.asarray(t) for t in host_tables())
    tw = tl.reshape(2, lat_parts, 24, lon_cells).transpose(1, 0, 2, 3).reshape(768, lon_cells)
    layers = mix_first.shape[0]
    current = field_in
    stats, bias = lax.optimization_barrier((first_stats(field_in), mix_bias.astype(F32)))
    band = pay = None
    for layer in range(layers):
        stats = swap(stats, CH)
        if layer == 0:
            normed, lon, band = norm_lon(layer, ln_gain, ln_shift, current, tw, stats)
        else:
            sums, pay = band_sums(stats, band)
            pay = swap(pay, LAT)
            normed, lon = norm_lon(layer, ln_gain, ln_shift, current, tw, sums, pay)
        back = spectral(layer, swap(lon, LAT), mix_first, bias, mix_second, tf, ti)
        first, last = layer == 0, layer == layers - 1
        extra = [] if first else [pay]
        current, stats = spatial(first, last, extra, swap(back, LAT), current, normed, tl)
    return final_scale(pay, swap(stats, LAT_CH), current)


def solution(mesh):
    finer = Mesh(mesh.devices.reshape(4, 4, 4, 2), LAT_CH)
    in_specs = (
        P(CH, LAT, None),
        P(None, CH),
        P(None, CH),
        P(None, None, CH, None, None),
        P(None, None, CH, None),
        P(None, None, CH, None, None),
    )
    return jax.shard_map(
        per_device, mesh=finer, in_specs=in_specs, out_specs=P(CH, LAT, None), check_vma=False
    )
```

time: 357 us -> 311 us (0.87)
  blocking collectives: 188 us -> 245 us
  waiting for transfers between devices: 53.3 us -> 0 us
  Pallas kernels: 94.4 us -> 62.3 us
  starting transfers between devices: 13.6 us -> 0 us
    all_to_all x6 -> x8, blocking collectives: 188 us -> 245 us  [swap(): return lax.all_to_all(x, axes, split_axis=0, concat_axis=0, tiled=True)]
    all_to_all x2 -> x0, waiting for transfers between devices: 53.3 us -> none  [swap(): return lax.all_to_all(x, axes, split_axis=0, concat_axis=0, tiled=True)]
    all_to_all x2 -> x0, starting transfers between devices: 13.6 us -> none  [swap(): return lax.all_to_all(x, axes, split_axis=0, concat_axis=0, tiled=True)]
    pallas_call x2, Pallas kernels: 42.9 us -> 31.7 us  [spectral(): pl.pallas_call(kernel, out_shape=jax.ShapeDtypeStruct(r.shape, BF16), in_...]
    pallas_call x2, Pallas kernels: 25.9 us -> 15.7 us  [spatial(): pl.pallas_call(kernel, out_shape=(jax.ShapeDtypeStruct(v.shape, BF16), st...]
    pallas_call x2, Pallas kernels: 17.7 us -> 10.1 us  [norm_lon(): pl.pallas_call(kernel, out_shape=tuple(outs), in_specs=[SM, SM] + [VM] *...]
  transfers between devices with their start and end apart: 2 -> 0, of which waited for: 2 -> 0; matrix products, arithmetic and copies ran while one was open for 0% -> 0% of each run, Pallas kernels for 0% -> 0%
where the time goes in v4:
time: 311 us; the launch traced here: 310 us
  blocking collectives  245 us (79%)
  Pallas kernels  62.3 us (20%)
    all_to_all x8, blocking collectives, swap(): return lax.all_to_all(x, axes, split_axis=0, concat_axis=0, tiled=True)  245 us
    pallas_call x2, Pallas kernels, spectral(): pl.pallas_call(kernel, out_shape=jax.ShapeDtypeStruct(r.shape, BF16), in_...  31.7 us
    pallas_call x2, Pallas kernels, spatial(): pl.pallas_call(kernel, out_shape=(jax.ShapeDtypeStruct(v.shape, BF16), st...  15.7 us
    pallas_call x2, Pallas kernels, norm_lon(): pl.pallas_call(kernel, out_shape=tuple(outs), in_specs=[SM, SM] + [VM] *...  10.1 us

profile of v4, /device:TPU:1, one launch (start us, length us, event | category | flops | bytes accessed | tf_op | source)
XLA Modules:
  0.0 310.2 jit_solution(16221996527083314688)
XLA Ops:
  0.0 0.0 copy-start.6
  0.0 0.0 copy-start.5
  0.0 0.7 copy_convert_fusion.refs_2_
  0.7 0.0 copy-start
  0.7 2.0 copy-done
  2.7 0.0 copy-start.1
  2.7 0.0 copy-start.7
  2.7 0.8 first_stats.1
  3.5 16.0 %all_to_all.40.refs_4_ = bf16[8,2,24,768]{3,2,1,0:T(8,128)(2,1)S(1)} all-to-all(bf16[8,2,24,768]{3,2,1,0:T(8,128)(2,1)S(1)} %first_stats.1), channel_id=1, replica_groups=mesh['lat_0'=4,'lat_1'=4,'ch_0'=4,'ch_1'=2] {'ch_0','ch_1'}, dimensions={0} | all-to-all | bytes 1179648 | tf_op jit(solution)/shard_map/all_to_all | solution.py:344
  19.5 0.0 copy-done.6
  19.5 0.0 copy-done.5
  19.6 0.0 copy-done.1
  19.6 0.0 copy-done.7
  19.6 5.1 %norm_lon.2 = (bf16[96,24,768]{2,1,0:T(8,128)(2,1)S(1)}, bf16[16,48,2304]{2,1,0:T(8,128)(2,1)S(1)}, f32[1,128]{1,0:T(1,128)S(1)}) custom-call(f32[2,96]{1,0:T(2,128)S(1)} %copy-done.5, f32[2,96]{1,0:T(2,128)S(1)} %copy-done.6, bf16[96,24,768]{2,1,0:T(8,128)(2,1)S(1)} %copy-done.1, bf16[768,768]{1,0:T(8,128)(2,1)S(1)} %copy-done.7, ...), custom_call_target="tpu_custom_call" | custom-call | flops 3000000000 | bytes 10000000 | tf_op jit(solution)/shard_map/norm_lon/pallas_call | solution.py:180
  24.7 0.0 copy-start.3
  24.7 0.0 copy-start.4
  24.7 0.0 copy-start.8
  24.7 0.0 copy-start.9
  24.7 50.0 %all_to_all.41.refs_0_ = bf16[16,48,2304]{2,1,0:T(8,128)(2,1)S(1)} all-to-all(bf16[16,48,2304]{2,1,0:T(8,128)(2,1)S(1)} %get-tuple-element.19), channel_id=1, replica_groups=mesh['lat_0'=4,'lat_1'=4,'ch_0'=4,'ch_1'=2] {'lat_0','lat_1'}, dimensions={0} | all-to-all | bytes 7077888 | tf_op jit(solution)/shard_map/all_to_all | solution.py:344
  74.7 0.0 copy-done.3
  74.7 0.0 copy-done.4
  74.7 0.0 copy-done.8
  74.7 0.0 copy-done.9
  74.8 15.9 %spectral.2 = bf16[16,48,2304]{2,1,0:T(8,128)(2,1)S(1)} custom-call(bf16[16,48,2304]{2,1,0:T(8,128)(2,1)S(1)} %all_to_all.41.refs_0_, bf16[2,2,1,96,96]{4,3,2,1,0:T(8,128)(2,1)S(1)} %copy-done.3, f32[2,2,1,96]{3,2,1,0:T(1,128)S(1)} %copy_convert_fusion.refs_2_, bf16[2,2,1,96,96]{4,3,2,1,0:T(8,128)(2,1)S(1)} %copy-done.4, bf16[384,768]{1,0:T(8,128)(2,1)S(1)} %copy-done.9, ...), custom_call_target="tpu_custom_call" | custom-call | flops 12000000000 | bytes 10000000 | tf_op jit(solution)/shard_map/spectral/pallas_call | solution.py:254
  90.6 0.0 copy-start.2
  90.6 45.7 %all_to_all.42.refs_0_ = bf16[16,48,2304]{2,1,0:T(8,128)(2,1)S(1)} all-to-all(bf16[16,48,2304]{2,1,0:T(8,128)(2,1)S(1)} %spectral.2), channel_id=1, replica_groups=mesh['lat_0'=4,'lat_1'=4,'ch_0'=4,'ch_1'=2] {'lat_0','lat_1'}, dimensions={0} | all-to-all | bytes 7077888 | tf_op jit(solution)/shard_map/all_to_all | solution.py:344
  136.3 0.0 copy-done.2
  136.3 7.7 %spatial.2 = (bf16[96,24,768]{2,1,0:T(8,128)(2,1)S(1)}, bf16[8,2,24,768]{3,2,1,0:T(8,128)(2,1)S(1)}) custom-call(bf16[16,48,2304]{2,1,0:T(8,128)(2,1)S(1)} %all_to_all.42.refs_0_, bf16[96,24,768]{2,1,0:T(8,128)(2,1)S(1)} %copy-done.1, bf16[96,24,768]{2,1,0:T(8,128)(2,1)S(1)} %get-tuple-element.21.refs_2_, bf16[768,768]{1,0:T(8,128)(2,1)S(1)} %copy-done.2), custom_call_target="tpu_custom_call" | custom-call | flops 3000000000 | bytes 15000000 | tf_op jit(solution)/shard_map/spatial/pallas_call | solution.py:310
  144.1 15.6 %all_to_all.43.st_ref = bf16[8,2,24,768]{3,2,1,0:T(8,128)(2,1)S(1)} all-to-all(bf16[8,2,24,768]{3,2,1,0:T(8,128)(2,1)S(1)} %get-tuple-element.22), channel_id=1, replica_groups=mesh['lat_0'=4,'lat_1'=4,'ch_0'=4,'ch_1'=2] {'ch_0','ch_1'}, dimensions={0} | all-to-all | bytes 1179648 | tf_op jit(solution)/shard_map/all_to_all | solution.py:344
  159.7 0.3 band_sums.1
  160.0 10.1 %all_to_all.44.refs_5_.refs_0_.pay_ref = f32[16,2,128]{2,1,0:T(2,128)S(1)} all-to-all(f32[16,2,128]{2,1,0:T(2,128)S(1)} %get-tuple-element.24), channel_id=1, replica_groups=mesh['lat_0'=4,'lat_1'=4,'ch_0'=4,'ch_1'=2] {'lat_0','lat_1'}, dimensions={0} | all-to-all | bytes 32768 | tf_op jit(solution)/shard_map/all_to_all | solution.py:344
  170.1 5.0 %norm_lon.3 = (bf16[96,24,768]{2,1,0:T(8,128)(2,1)S(1)}, bf16[16,48,2304]{2,1,0:T(8,128)(2,1)S(1)}) custom-call(f32[2,96]{1,0:T(2,128)S(1)} %copy-done.5, f32[2,96]{1,0:T(2,128)S(1)} %copy-done.6, bf16[96,24,768]{2,1,0:T(8,128)(2,1)S(1)} %get-tuple-element.25.refs_2_, bf16[768,768]{1,0:T(8,128)(2,1)S(1)} %copy-done.7, ...), custom_call_target="tpu_custom_call" | custom-call | flops 3000000000 | bytes 10000000 | tf_op jit(solution)/shard_map/norm_lon/pallas_call | solution.py:180
  175.1 44.6 %all_to_all.45.refs_0_ = bf16[16,48,2304]{2,1,0:T(8,128)(2,1)S(1)} all-to-all(bf16[16,48,2304]{2,1,0:T(8,128)(2,1)S(1)} %get-tuple-element.27), channel_id=1, replica_groups=mesh['lat_0'=4,'lat_1'=4,'ch_0'=4,'ch_1'=2] {'lat_0','lat_1'}, dimensions={0} | all-to-all | bytes 7077888 | tf_op jit(solution)/shard_map/all_to_all | solution.py:344
  219.6 15.8 %spectral.3 = bf16[16,48,2304]{2,1,0:T(8,128)(2,1)S(1)} custom-call(bf16[16,48,2304]{2,1,0:T(8,128)(2,1)S(1)} %all_to_all.45.refs_0_, bf16[2,2,1,96,96]{4,3,2,1,0:T(8,128)(2,1)S(1)} %copy-done.3, f32[2,2,1,96]{3,2,1,0:T(1,128)S(1)} %copy_convert_fusion.refs_2_, bf16[2,2,1,96,96]{4,3,2,1,0:T(8,128)(2,1)S(1)} %copy-done.4, bf16[384,768]{1,0:T(8,128)(2,1)S(1)} %copy-done.9, ...), custom_call_target="tpu_custom_call" | custom-call | flops 12000000000 | bytes 10000000 | tf_op jit(solution)/shard_map/spectral/pallas_call | solution.py:254
  235.5 47.2 %all_to_all.46.refs_1_ = bf16[16,48,2304]{2,1,0:T(8,128)(2,1)S(1)} all-to-all(bf16[16,48,2304]{2,1,0:T(8,128)(2,1)S(1)} %spectral.3), channel_id=1, replica_groups=mesh['lat_0'=4,'lat_1'=4,'ch_0'=4,'ch_1'=2] {'lat_0','lat_1'}, dimensions={0} | all-to-all | bytes 7077888 | tf_op jit(solution)/shard_map/all_to_all | solution.py:344
  282.7 7.9 %spatial.3 = (bf16[96,24,768]{2,1,0:T(8,128)(2,1)S(1)}, f32[128,1,128]{2,1,0:T(1,128)S(1)}) custom-call(f32[16,2,128]{2,1,0:T(2,128)S(1)} %all_to_all.44.refs_5_.refs_0_.pay_ref, bf16[16,48,2304]{2,1,0:T(8,128)(2,1)S(1)} %all_to_all.46.refs_1_, bf16[96,24,768]{2,1,0:T(8,128)(2,1)S(1)} %get-tuple-element.25.refs_2_, ...), custom_call_target="tpu_custom_call" | custom-call | flops 3000000000 | bytes 15000000 | tf_op jit(solution)/shard_map/spatial/pallas_call | solution.py:310
  290.6 15.7 %all_to_all.47.energy_ref = f32[128,1,128]{2,1,0:T(1,128)S(1)} all-to-all(f32[128,1,128]{2,1,0:T(1,128)S(1)} %get-tuple-element.29), channel_id=1, replica_groups=mesh['lat_0'=4,'lat_1'=4,'ch_0'=4,'ch_1'=2] {'lat_0','lat_1','ch_0','ch_1'}, dimensions={0} | all-to-all | bytes 131072 | tf_op jit(solution)/shard_map/all_to_all | solution.py:344
  306.3 3.8 %final_scale.1 = bf16[96,24,768]{2,1,0:T(8,128)(2,1)} custom-call(f32[16,2,128]{2,1,0:T(2,128)S(1)} %all_to_all.44.refs_5_.refs_0_.pay_ref, f32[128,1,128]{2,1,0:T(1,128)S(1)} %all_to_all.47.energy_ref, bf16[96,24,768]{2,1,0:T(8,128)(2,1)S(1)} %get-tuple-element.30.u_ref), custom_call_target="tpu_custom_call" | custom-call | flops 10000000 | bytes 7000000 | tf_op jit(solution)/shard_map/final_scale/pallas_call | solution.py:331
Async XLA Ops:
  0.0 19.5 %copy-start.6 = (f32[2,96]{1,0:T(2,128)S(1)}, f32[2,96]{1,0:T(2,128)}, u32[]{:S(2)}) copy-start(f32[2,96]{1,0:T(2,128)} %refs_1_.8) | copy-start | bytes 2308
  0.0 19.5 %copy-start.5 = (f32[2,96]{1,0:T(2,128)S(1)}, f32[2,96]{1,0:T(2,128)}, u32[]{:S(2)}) copy-start(f32[2,96]{1,0:T(2,128)} %refs_0_.3) | copy-start | bytes 2308
  0.7 2.0 copy-start
  2.7 16.8 %copy-start.1 = (bf16[96,24,768]{2,1,0:T(8,128)(2,1)S(1)}, bf16[96,24,768]{2,1,0:T(8,128)(2,1)}, u32[]{:S(2)}) copy-start(bf16[96,24,768]{2,1,0:T(8,128)(2,1)} %refs_1_.7) | copy-start | bytes 10616836
  2.7 16.8 %copy-start.7 = (bf16[768,768]{1,0:T(8,128)(2,1)S(1)}, bf16[768,768]{1,0:T(8,128)(2,1)}, u32[]{:S(2)}) copy-start(bf16[768,768]{1,0:T(8,128)(2,1)} %constant.15.refs_3_) | copy-start | bytes 3538948
  24.7 50.1 %copy-start.3 = (bf16[2,2,1,96,96]{4,3,2,1,0:T(8,128)(2,1)S(1)}, bf16[2,2,1,96,96]{4,3,2,1,0:T(8,128)(2,1)}, u32[]{:S(2)}) copy-start(bf16[2,2,1,96,96]{4,3,2,1,0:T(8,128)(2,1)} %refs_1_.9) | copy-start | bytes 221188
  24.7 50.0 %copy-start.4 = (bf16[2,2,1,96,96]{4,3,2,1,0:T(8,128)(2,1)S(1)}, bf16[2,2,1,96,96]{4,3,2,1,0:T(8,128)(2,1)}, u32[]{:S(2)}) copy-start(bf16[2,2,1,96,96]{4,3,2,1,0:T(8,128)(2,1)} %refs_3_.4) | copy-start | bytes 221188
  24.7 50.0 %copy-start.8 = (bf16[768,768]{1,0:T(8,128)(2,1)S(1)}, bf16[768,768]{1,0:T(8,128)(2,1)}, u32[]{:S(2)}) copy-start(bf16[768,768]{1,0:T(8,128)(2,1)} %constant.7.clone.refs_5_) | copy-start | bytes 3538948
  24.7 50.0 %copy-start.9 = (bf16[384,768]{1,0:T(8,128)(2,1)S(1)}, bf16[384,768]{1,0:T(8,128)(2,1)}, u32[]{:S(2)}) copy-start(bf16[384,768]{1,0:T(8,128)(2,1)} %constant.6.clone.refs_4_) | copy-start | bytes 1769476
  90.6 45.7 %copy-start.2 = (bf16[768,768]{1,0:T(8,128)(2,1)S(1)}, bf16[768,768]{1,0:T(8,128)(2,1)}, u32[]{:S(2)}) copy-start(bf16[768,768]{1,0:T(8,128)(2,1)} %constant.8.clone.refs_3_.refs_4_) | copy-start | bytes 3538948
